TPU v7x, 512 devices: a whole 4x8x8 slice. The times are simulated.
512 devices in a mesh: blk: 32 (over x, y), grp: 16 (over z, core).
Axes of the slice: x: 4, y: 8, z: 8, core: 2. Of those that a mesh axis runs over, the one named last changes fastest.
Arguments:
- queries: bfloat16 [192, 8192], P(None, ('blk', 'grp')), may hold values from -6 to 6
- key_pool: bfloat16 [16, 256, 128, 1024], P('grp', 'blk'), may hold values from -28 to 28
- value_pool: bfloat16 [16, 256, 128, 1024], P('grp', 'blk'), may hold values from -6 to 6
- lengths: int32 [16, 4], P('grp'), may hold values from 1 to 128, as said below
- block_table: int32 [16, 4, 128], P('grp'), may hold values from 0 to 255, as said below
Outputs:
- attended: bfloat16 [192, 8192], P('grp', 'blk')
Inputs may be any that keep to these rules, and one draw needn't show every extreme that they name: Each group's 4 lengths add up to 208, and one of them is exactly 128. Within a group, the entries block_table[g, q, j] with j < lengths[g, q] are distinct slots; entries past a sequence's length are arbitrary slots and unused. Slots s * 8 to s * 8 + 7 form the s-th aligned block of the pool; at least 4 and at most 8 live slots lie in one aligned block, and exactly 8 in some aligned block of every group.
All inputs are finite; a program needn't handle non-finite values.
Results may differ from a plain program's by a relative error of at most 0.0049.
Values may be sent and summed in bfloat16 or wider, within the bound.
No kernel may reach another device: no remote copies, remote signals or barrier semaphores. Data moves between devices by JAX's collectives and lax.ppermute only.
A program may use at most 64 MiB of HBM per device.

v0:
```python
import math

import jax
import jax.numpy as jnp
from jax import lax
from jax.sharding import PartitionSpec as P

HQ = 64
KVH = 8
DH = 128
STEPS = 3


empty_max = -1e30


def in_order(pieces, dim):
    pieces = jnp.moveaxis(pieces, 0, dim)
    dims = pieces.shape
    return pieces.reshape(*dims[:dim], dims[dim] * dims[dim + 1], *dims[dim + 2 :])


def sent_to_all(shard, axis):
    copies = jnp.broadcast_to(shard, (lax.axis_size(axis), *shard.shape))
    return lax.all_to_all(copies, axis, split_axis=0, concat_axis=0, tiled=True)


def gather_directly(shard, axis, dim):
    return in_order(sent_to_all(shard, axis), dim)


def in_one_piece(arrays, axis, split_dim, concat_dim, along):
    widths = [math.prod(a.shape[along:]) for a in arrays]
    both = jnp.concatenate(
        [a.reshape(*a.shape[:along], w) for a, w in zip(arrays, widths)], axis=along
    )
    filled = lax.all_to_all(both, axis, split_axis=split_dim, concat_axis=concat_dim, tiled=True)
    pieces = jnp.split(filled, [sum(widths[:k]) for k in range(1, len(widths))], axis=along)
    return tuple(
        (b.reshape(*filled.shape[:along], *a.shape[along:]) for a, b in zip(arrays, pieces))
    )


def owners(seq_lengths, slot_table, first_slot, slot_count):
    slot_ids = first_slot + jnp.arange(slot_count, dtype=jnp.int32)
    places = jnp.arange(slot_table.shape[1], dtype=jnp.int32)
    in_length = places[None, :] < seq_lengths[:, None]
    matches = (slot_table[:, :, None] == slot_ids[None, None, :]) & in_length[:, :, None]
    return jnp.transpose(jnp.any(matches, axis=1))


def slot_partials(query_block, key_block, value_block):
    slot_count = key_block.shape[0]
    per_group = HQ // KVH
    grouped_q = query_block.reshape(slot_count, STEPS, KVH, per_group, DH)
    grouped_q = jnp.transpose(grouped_q, (0, 2, 1, 3, 4)).reshape(
        slot_count, KVH, STEPS * per_group, DH
    )
    key_heads = key_block.reshape(slot_count, key_block.shape[1], KVH, DH)
    value_heads = value_block.reshape(slot_count, value_block.shape[1], KVH, DH)
    scores = jnp.einsum(
        "cgqd,ctgd->cgqt", grouped_q, key_heads, preferred_element_type=jnp.float32
    ) * (1.0 / math.sqrt(DH))
    block_max = jnp.max(scores, axis=3)
    weights = jnp.exp(scores - block_max[..., None]).astype(jnp.bfloat16)
    block_total = jnp.sum(weights.astype(jnp.float32), axis=3)
    block_out = jnp.einsum(
        "cgqt,ctgd->cgqd", weights, value_heads, preferred_element_type=jnp.float32
    )
    return (block_max, block_total, block_out)


def gather_sequences(owned, block_max, block_total, block_out):
    masked = jnp.where(owned[:, :, None, None], block_max[:, None], empty_max)
    seq_max = jnp.max(masked, axis=0)
    factor = jnp.where(owned[:, :, None, None], jnp.exp(block_max[:, None] - seq_max[None]), 0.0)
    seq_total = jnp.sum(factor * block_total[:, None], axis=0)
    seq_out = jnp.einsum("cqgh,cghd->qghd", factor, block_out, precision=lax.Precision.HIGHEST)
    seq_count = owned.shape[1]
    per_group = HQ // KVH
    seq_max = jnp.transpose(
        seq_max.reshape(seq_count, KVH, STEPS, per_group), (0, 2, 1, 3)
    ).reshape(seq_count * STEPS, HQ)
    seq_total = jnp.transpose(
        seq_total.reshape(seq_count, KVH, STEPS, per_group), (0, 2, 1, 3)
    ).reshape(seq_count * STEPS, HQ)
    seq_out = jnp.transpose(
        seq_out.reshape(seq_count, KVH, STEPS, per_group, DH), (0, 2, 1, 3, 4)
    ).reshape(seq_count * STEPS, HQ, DH)
    return (seq_max, seq_total, seq_out)


def block_summary(owned, query_seq, key_block, value_block):
    query_block = jnp.dot(
        owned.astype(jnp.bfloat16), query_seq, preferred_element_type=jnp.float32
    ).astype(jnp.bfloat16)
    block_max, block_total, block_out = slot_partials(query_block, key_block, value_block)
    return gather_sequences(owned, block_max, block_total, block_out)


def body(queries, key_pool, value_pool, lengths, block_table):
    grouped = lax.all_to_all(queries, "grp", split_axis=0, concat_axis=1, tiled=True)
    query_full = gather_directly(grouped, "blk", 1)
    token_count = query_full.shape[0]
    query_seq = query_full.reshape(token_count // STEPS, STEPS * query_full.shape[1])
    local_keys = key_pool[0]
    local_values = value_pool[0]
    slots_here = local_keys.shape[0]
    first_slot = lax.axis_index("blk") * slots_here
    owned = owners(lengths[0], block_table[0], first_slot, slots_here)
    seq_max, seq_total, seq_out = block_summary(owned, query_seq, local_keys, local_values)
    cycle_size = lax.axis_size("blk")
    heads_here = HQ // cycle_size
    arrived_max, arrived_total, arrived_out = in_one_piece(
        (seq_max[None], seq_total[None], seq_out[None]), "blk", 2, 0, 3
    )
    slice_max = jnp.max(arrived_max, axis=0)
    scaling = jnp.exp(arrived_max - slice_max[None])
    mine_total = jnp.sum(scaling * arrived_total, axis=0)
    mine_out = jnp.sum(scaling[..., None] * arrived_out, axis=0)
    attended = (mine_out / mine_total[..., None]).astype(jnp.bfloat16)
    return attended.reshape(mine_out.shape[0], heads_here * DH)


def solution(mesh):
    placed = (
        P(None, ("blk", "grp")),
        P("grp", "blk", None, None),
        P("grp", "blk", None, None),
        P("grp", None),
        P("grp", None, None),
    )
    return jax.shard_map(
        body, mesh=mesh, in_specs=placed, out_specs=P("grp", "blk"), check_vma=False
    )
```

profile of v0, /device:TPU:8, one launch (start us, length us, event | category | flops | bytes accessed | tf_op | source)
XLA Modules:
  0.0 86.1 jit_solution(13044851202218777245)
XLA Ops:
  0.0 0.8 all_to_all.30
  0.8 0.6 copy.143
  1.5 10.4 %all-to-all-start = ((bf16[16,12,16]{1,2,0:T(8,128)(2,1)}), bf16[16,12,16]{1,2,0:T(8,128)(2,1)S(1)}, u32[]{:S(2)}, u32[]{:S(2)}) async-start(bf16[16,12,16]{1,2,0:T(8,128)(2,1)} %copy.143), calls=%async_computation | async-start | bytes 131072 | tf_op jit(solution)/shard_map/all_to_all | solution.py:102
  11.9 7.8 %all-to-all-done = bf16[16,12,16]{1,2,0:T(8,128)(2,1)S(1)} async-done(((bf16[16,12,16]{1,2,0:T(8,128)(2,1)}), bf16[16,12,16]{1,2,0:T(8,128)(2,1)S(1)}, u32[]{:S(2)}, u32[]{:S(2)}) %all-to-all-start) | async-done | bytes 6176 | tf_op jit(solution)/shard_map/all_to_all | solution.py:102
  19.7 0.1 copy.164
  19.8 0.8 broadcast_in_dim.33
  20.5 10.2 %all-to-all-start.1 = ((bf16[32,12,256]{2,1,0:T(8,128)(2,1)}), bf16[32,12,256]{2,1,0:T(8,128)(2,1)S(1)}, u32[]{:S(2)}, u32[]{:S(2)}) async-start(bf16[32,12,256]{2,1,0:T(8,128)(2,1)} %broadcast_in_dim.33), calls=%async_computation.1 | async-start | bytes 524288 | tf_op jit(solution)/shard_map/all_to_all | solution.py:25
  30.7 0.0 copy-start
  30.7 3.7 %copy.169 = bf16[128,8,8,128]{3,2,1,0:T(8,128)(2,1)} copy(bf16[128,8,8,128]{3,1,2,0:T(8,128)(2,1)} %bitcast.71) | data formatting | bytes 4194304
  34.4 0.0 copy-done
  34.4 0.0 copy-start.4
  34.4 0.0 copy-start.3
  34.4 0.6 copy.170
  35.1 0.0 copy-done.4
  35.1 0.1 iota_compare_fusion
  35.2 0.0 copy-done.3
  35.2 0.2 and_reduce_fusion
  35.4 0.0 copy-start.1
  35.4 8.1 %all-to-all-done.1 = bf16[32,12,256]{2,1,0:T(8,128)(2,1)S(1)} async-done(((bf16[32,12,256]{2,1,0:T(8,128)(2,1)}), bf16[32,12,256]{2,1,0:T(8,128)(2,1)S(1)}, u32[]{:S(2)}, u32[]{:S(2)}) %all-to-all-start.1) | async-done | bytes 196640 | tf_op jit(solution)/shard_map/all_to_all | solution.py:25
  43.5 0.1 copy.145
  43.6 0.1 reshape_reshape.3
  43.7 0.3 convolution_convert_fusion
  44.0 2.9 %fusion.20 = (f32[8,8,24]{2,1,0:T(8,128)S(1)}, f32[8,8,24,128]{3,2,1,0:T(8,128)S(1)}) fusion(bf16[8,128,8,128]{3,2,1,0:T(8,128)(2,1)} %bitcast.65, bf16[8,8,3,8,128]{4,0,3,1,2:T(8,128)(2,1)S(1)} %bitcast.73), kind=kOutput, calls=%fused_computation.34 | convolution fusion | flops 50723328 | bytes 3282944 | tf_op jit(solution)/shard_map/cgqd,ctgd->cgqt/dot_general | solution.py:61
  46.9 0.1 copy.148
  47.0 0.5 convert_reduce_fusion
  47.5 0.1 copy.151
  47.6 0.3 select_reduce_fusion
  47.9 0.0 copy-done.1
  47.9 0.5 multiply_reduce_fusion
  48.5 0.3 copy.166
  48.8 0.2 reshape_broadcast_in_dim_reshape.9
  48.9 0.0 copy-start.2
  49.0 0.7 fusion
  49.7 0.0 copy-done.2
  49.7 1.9 %fusion.8 = f32[8,24,128,4]{2,3,1,0:T(4,128)S(1)} fusion(f32[8,8,24,128]{3,2,1,0:T(8,128)S(1)} %fusion, f32[4,8,24]{0,2,1:T(8,128)S(1)} %select_reduce_fusion, f32[8,8,24]{0,2,1:T(8,128)S(1)} %copy.148, pred[8,4]{0,1:T(4,128)(4,1)S(1)} %bitcast.85), kind=kOutput, calls=%fused_computation.9 | convolution fusion | flops 9449472 | bytes 1188896 | tf_op jit(solution)/shard_map/cqgh,cghd->qghd/dot_general | solution.py:78
  51.6 0.3 copy.165
  51.9 0.2 reshape_broadcast_in_dim_reshape.8
  52.1 0.5 pad_maximum_fusion
  52.6 0.8 copy.159
  53.4 27.4 %all_to_all.42 = f32[1,12,64,130]{3,0,1,2:T(1,128)S(1)} all-to-all(f32[1,12,64,130]{3,0,1,2:T(1,128)S(1)} %copy.159), channel_id=1, replica_groups=mesh['blk'=32,'grp'=16] {'blk'}, dimensions={2} | all-to-all | bytes 798720 | tf_op jit(solution)/shard_map/all_to_all | solution.py:37
  80.7 0.7 copy.160
  81.5 1.5 %copy.161 = f32[1,12,32,2,130]{2,3,4,1,0:T(2,128)S(1)} copy(f32[1,12,32,2,130]{4,0,3,2,1:T(1,128)S(1)} %bitcast.70) | data formatting | bytes 798720 | tf_op jit(solution)/shard_map/all_to_all | solution.py:37
  83.0 0.1 slice_reduce_fusion
  83.1 0.2 fusion.17
  83.3 0.1 exponential_bitcast_fusion
  83.4 1.7 %fusion.4 = f32[12,2,128]{1,2,0:T(8,128)S(1)} fusion(f32[32,12,2,130]{0,2,3,1:T(2,128)S(1)} %bitcast.69, f32[32,12,2]{0,2,1:T(2,128)S(1)} %exponential_bitcast_fusion), kind=kLoop, calls=%fused_computation.6 | loop fusion | flops 193536 | bytes 408576 | tf_op jit(solution)/shard_map/reduce_sum | solution.py:120
  85.1 0.3 copy.163
  85.3 0.1 divide_convert_fusion
  85.5 0.6 copy.171
  (5 shorter events, 0.1 us)
Async XLA Ops:
  1.5 18.2 %all-to-all-start = ((bf16[16,12,16]{1,2,0:T(8,128)(2,1)}), bf16[16,12,16]{1,2,0:T(8,128)(2,1)S(1)}, u32[]{:S(2)}, u32[]{:S(2)}) async-start(bf16[16,12,16]{1,2,0:T(8,128)(2,1)} %copy.143), calls=%async_computation | async-start | bytes 131072 | tf_op jit(solution)/shard_map/all_to_all | solution.py:102
  20.5 23.0 %all-to-all-start.1 = ((bf16[32,12,256]{2,1,0:T(8,128)(2,1)}), bf16[32,12,256]{2,1,0:T(8,128)(2,1)S(1)}, u32[]{:S(2)}, u32[]{:S(2)}) async-start(bf16[32,12,256]{2,1,0:T(8,128)(2,1)} %broadcast_in_dim.33), calls=%async_computation.1 | async-start | bytes 524288 | tf_op jit(solution)/shard_map/all_to_all | solution.py:25
  30.7 3.7 %copy-start = (bf16[1,8,128,1024]{3,2,1,0:T(8,128)(2,1)S(1)}, bf16[1,8,128,1024]{3,2,1,0:T(8,128)(2,1)}, u32[]{:S(2)}) copy-start(bf16[1,8,128,1024]{3,2,1,0:T(8,128)(2,1)} %param.7) | copy-start | bytes 6291460
  34.4 0.7 copy-start.4
  34.4 0.7 copy-start.3
  35.4 12.5 %copy-start.1 = (pred[4,8]{1,0:T(4,128)(4,1)}, pred[4,8]{1,0:T(4,128)(4,1)S(1)}, u32[]{:S(2)}) copy-start(pred[4,8]{1,0:T(4,128)(4,1)S(1)} %and_reduce_fusion) | copy-start | bytes 100
  48.9 0.7 copy-start.2
where the time goes:
time: 86.4 us; the launch traced here: 86.1 us
  blocking collectives  27.4 us (32%)
  starting transfers between devices  20.6 us (24%)
  waiting for transfers between devices  15.9 us (18%)
  local copies, waits for them, and re-layouts  12 us (14%)
  matrix products  5.78 us (7%)
  other arithmetic  4.24 us (5%)
    all_to_all x1, blocking collectives, in_one_piece(): lax.all_to_all(both, axis, split_axis=split_dim, concat_axis=concat_dim,...  27.4 us
    all_to_all x1, starting transfers between devices, body(): lax.all_to_all(queries, 'grp', split_axis=0, concat_axis=1, tiled=True)  10.4 us
    all_to_all x1, starting transfers between devices, sent_to_all(): return lax.all_to_all(copies, axis, split_axis=0, concat_axis=0, tiled=True)  10.2 us
    all_to_all x1, waiting for transfers between devices, sent_to_all(): return lax.all_to_all(copies, axis, split_axis=0, concat_axis=0, tiled=True)  8.12 us
    all_to_all x1, waiting for transfers between devices, body(): lax.all_to_all(queries, 'grp', split_axis=0, concat_axis=1, tiled=True)  7.79 us
    unnamed x14, local copies, waits for them, and re-layouts  5 us
    dot_general x1, matrix products, slot_partials(): jnp.einsum('cgqd,ctgd->cgqt', grouped_q, key_heads, preferred_element_typ...  2.87 us
    all_to_all x2, local copies, waits for them, and re-layouts, in_one_piece(): lax.all_to_all(both, axis, split_axis=split_dim, concat_axis=concat_dim,...  2.26 us
  transfers between devices with their start and end apart: 2, of which 2 were waited for; matrix products, arithmetic and copies ran while one was open for 5% of the time, Pallas kernels for 0%

commit v1 on v0

v1 whole, which is shorter than its diff:
```python
import math

import jax
import jax.numpy as jnp
from jax import lax
from jax.experimental import pallas as pl
from jax.experimental.pallas import tpu as pltpu
from jax.sharding import PartitionSpec as P

HQ = 64
KVH = 8
DH = 128
STEPS = 3
SEQS = 4
TOK = SEQS * STEPS
HEADS = 2
ROWS = HEADS * TOK
SLICES = 4
SLOTS = 8
BLOCK = 128
LANES = 128
SCALE = math.log2(math.e) / math.sqrt(DH)
LN2 = math.log(2.0)
EMPTY = -1e30

VMEM = pl.BlockSpec(memory_space=pltpu.VMEM)
SMEM = pl.BlockSpec(memory_space=pltpu.SMEM)


def iota(shape, dim):
    return lax.broadcasted_iota(jnp.int32, shape, dim)


def pack_kernel(q_ref, out_ref):
    groups, feats, _ = out_ref.shape
    q = q_ref[...].astype(jnp.float32)
    keep = iota((feats, LANES), 1) < TOK
    wide = jnp.concatenate([q, jnp.zeros((feats, 2 * LANES - q.shape[1]), jnp.float32)], axis=1)
    for g in range(groups):
        at = g * TOK
        shifted = wide if at == 0 else pltpu.roll(wide, 2 * LANES - at, 1)
        out_ref[g] = jnp.where(keep, shifted[:, :LANES], 0.0).astype(out_ref.dtype)


def spread_kernel(a_ref, out_ref):
    row = iota((ROWS, LANES), 0)
    tok = jnp.where(row >= TOK, row - TOK, row)
    pick = (tok == iota((ROWS, LANES), 1)).astype(jnp.bfloat16)
    nt = (((1,), (1,)), ((), ()))
    first = lax.dot_general(pick, a_ref[:LANES, :], nt, preferred_element_type=jnp.float32)
    second = lax.dot_general(pick, a_ref[LANES:, :], nt, preferred_element_type=jnp.float32)
    rows = jnp.where(row < TOK, first, second).astype(out_ref.dtype)
    for b in range(out_ref.shape[0]):
        out_ref[b] = rows


def attend_kernel(first_ref, len_ref, table_ref, q_ref, k_ref, v_ref, out_ref):
    lane4 = iota((SEQS, LANES), 1)
    sub4 = iota((SEQS, LANES), 0)
    lens = jnp.zeros((SEQS, LANES), jnp.int32)
    for q in range(SEQS):
        lens = jnp.where(sub4 == q, len_ref[0, q], lens)
    local = jnp.where(lane4 < lens, table_ref[...] - first_ref[0], -1)
    row = iota((ROWS, LANES), 0)
    seq = jnp.where(row >= TOK, row - TOK, row) // STEPS
    bias = []
    for s in range(SLOTS):
        hit = jnp.max((local == s).astype(jnp.float32), axis=1, keepdims=True)
        off = jnp.broadcast_to(jnp.where(hit > 0.0, 0.0, EMPTY), (SEQS, LANES))
        b = jnp.broadcast_to(off[0:1], (ROWS, LANES))
        for q in range(1, SEQS):
            b = jnp.where(seq == q, off[q : q + 1], b)
        bias.append(b)
    bias = jnp.concatenate(bias, axis=1)
    bias = jnp.concatenate([bias] * SLICES, axis=0)

    rows = SLICES * ROWS
    lane = iota((rows, LANES), 1)
    lse = jnp.zeros((rows, LANES), jnp.float32)
    nt = (((1,), (1,)), ((), ()))
    nn = (((1,), (0,)), ((), ()))
    for k in range(KVH):
        cols = slice(k * DH, (k + 1) * DH)
        qk = q_ref[k * SLICES : (k + 1) * SLICES].reshape(rows, DH)
        s = lax.dot_general(qk, k_ref[:, cols], nt, preferred_element_type=jnp.float32) + bias
        top = jnp.max(s, axis=1, keepdims=True)
        p = jnp.exp2((s - top) * SCALE).astype(jnp.bfloat16)
        total = jnp.sum(p.astype(jnp.float32), axis=1, keepdims=True)
        o = lax.dot_general(p, v_ref[:, cols], nn, preferred_element_type=jnp.float32)
        o = (o / total).astype(out_ref.dtype)
        lse = jnp.where(lane == k, top * SCALE + jnp.log2(total), lse)
        out_ref[k * SLICES : (k + 1) * SLICES, :ROWS, :] = o.reshape(SLICES, ROWS, DH)
    square = jnp.concatenate([lse, jnp.zeros((LANES - rows, LANES), jnp.float32)], axis=0)
    flat = jnp.transpose(square)[:KVH]
    lane8 = iota((KVH, LANES), 1)
    for j in range(SLICES):
        mine = flat if j == 0 else pltpu.roll(flat, LANES - j * ROWS, 1)
        mine = jnp.where(lane8 < ROWS, mine, 0.0)
        high = mine.astype(jnp.bfloat16).astype(jnp.float32)
        rest = mine - high
        mid = rest.astype(jnp.bfloat16).astype(jnp.float32)
        low = rest - mid
        line = high + pltpu.roll(mid, 32, 1) + pltpu.roll(low, 64, 1)
        for k in range(KVH):
            tile = jnp.broadcast_to(line[k : k + 1], (8, LANES))
            out_ref[k * SLICES + j, ROWS:, :] = tile.astype(out_ref.dtype)


def combine_kernel(a_ref, out_ref):
    devices = a_ref.shape[0]
    sub8 = iota((8, LANES), 0)
    parts = []
    for t in range(devices // 8):
        acc = a_ref[8 * t, ROWS:, :].astype(jnp.float32)
        for j in range(1, 8):
            acc = jnp.where(sub8 == j, a_ref[8 * t + j, ROWS:, :].astype(jnp.float32), acc)
        parts.append(acc)
    stat = jnp.concatenate(parts, axis=0)
    lse = stat + pltpu.roll(stat, LANES - 32, 1) + pltpu.roll(stat, LANES - 64, 1)
    top = jnp.max(lse, axis=0, keepdims=True)
    w = jnp.exp2(lse - top)
    w = w / jnp.sum(w, axis=0, keepdims=True)
    square = jnp.concatenate([w, jnp.zeros((LANES - devices, LANES), jnp.float32)], axis=0)
    wt = jnp.transpose(square)[:ROWS]
    acc = jnp.zeros((ROWS, LANES), jnp.float32)
    for b in range(devices):
        acc = acc + wt[:, b : b + 1] * a_ref[b, :ROWS, :].astype(jnp.float32)
    out_ref[...] = jnp.concatenate([acc[:TOK], acc[TOK:]], axis=1).astype(out_ref.dtype)


def body(queries, key_pool, value_pool, lengths, block_table):
    bf16 = jnp.bfloat16
    groups = lax.axis_size("grp")
    devices = lax.axis_size("blk")
    feats = queries.shape[1]
    packed = pl.pallas_call(
        pack_kernel,
        out_shape=jax.ShapeDtypeStruct((groups, feats, LANES), bf16),
        in_specs=[VMEM],
        out_specs=VMEM,
        name="pack",
    )(queries.T)
    arrived = lax.all_to_all(packed, "grp", split_axis=0, concat_axis=0, tiled=True)
    spread = pl.pallas_call(
        spread_kernel,
        out_shape=jax.ShapeDtypeStruct((devices, ROWS, LANES), bf16),
        in_specs=[VMEM],
        out_specs=VMEM,
        name="spread",
    )(arrived.reshape(groups * feats, LANES))
    query_all = lax.all_to_all(spread, "blk", split_axis=0, concat_axis=0, tiled=True)
    first = (lax.axis_index("blk") * SLOTS).astype(jnp.int32).reshape(1)
    partial = pl.pallas_call(
        attend_kernel,
        out_shape=jax.ShapeDtypeStruct((devices, ROWS + 8, LANES), bf16),
        in_specs=[SMEM, SMEM, VMEM, VMEM, VMEM, VMEM],
        out_specs=VMEM,
        name="attend",
    )(
        first,
        lengths,
        block_table[0],
        query_all,
        key_pool.reshape(SLOTS * BLOCK, KVH * DH),
        value_pool.reshape(SLOTS * BLOCK, KVH * DH),
    )
    collected = lax.all_to_all(partial, "blk", split_axis=0, concat_axis=0, tiled=True)
    return pl.pallas_call(
        combine_kernel,
        out_shape=jax.ShapeDtypeStruct((TOK, HEADS * DH), bf16),
        in_specs=[VMEM],
        out_specs=VMEM,
        name="combine",
    )(collected)


def solution(mesh):
    placed = (
        P(None, ("blk", "grp")),
        P("grp", "blk", None, None),
        P("grp", "blk", None, None),
        P("grp", None),
        P("grp", None, None),
    )
    return jax.shard_map(
        body, mesh=mesh, in_specs=placed, out_specs=P("grp", "blk"), check_vma=False
    )
```

time: 86.4 us -> 68.8 us (0.80)
  local copies, waits for them, and re-layouts: 12 us -> 0.69 us
  Pallas kernels: 0 us -> 11.2 us
  starting transfers between devices: 20.6 us -> 10.2 us
  blocking collectives: 27.4 us -> 34.8 us
  matrix products: 5.78 us -> 0 us
  waiting for transfers between devices: 15.9 us -> 11.5 us
  other arithmetic: 4.24 us -> 0 us
    pallas_call x0 -> x4, Pallas kernels: none -> 11.2 us  [the longest x1 6.14 us: body(): pl.pallas_call(attend_kernel, out_shape=jax.ShapeDtypeStruct((devices, RO...]
    all_to_all x2 -> x1, starting transfers between devices: 20.6 us -> 10.2 us  [body(): lax.all_to_all(spread, 'blk', split_axis=0, concat_axis=0, tiled=True)]
    all_to_all x1 -> x2, blocking collectives: 27.4 us -> 34.8 us  [the longest x1 18.3 us: body(): lax.all_to_all(packed, 'grp', split_axis=0, concat_axis=0, tiled=True)]
    dot_general x4 -> x0, matrix products: 5.78 us -> none  [the longest x1 2.87 us: slot_partials(): jnp.einsum('cgqd,ctgd->cgqt', grouped_q, key_heads, preferred_element_typ...]
    all_to_all x2 -> x1, waiting for transfers between devices: 15.9 us -> 11.5 us  [body(): lax.all_to_all(spread, 'blk', split_axis=0, concat_axis=0, tiled=True)]
    unnamed x14 -> x2, local copies, waits for them, and re-layouts: 5 us -> 0.69 us
    all_to_all x5 -> x0, local copies, waits for them, and re-layouts: 3.78 us -> none  [the longest x2 2.26 us: in_one_piece(): lax.all_to_all(both, axis, split_axis=split_dim, concat_axis=concat_dim,...]
    reduce_sum x4 -> x0, other arithmetic: 2.93 us -> none  [the longest x1 1.71 us: body(): mine_out = jnp.sum(scaling[..., None] * arrived_out, axis=0)]
  transfers between devices with their start and end apart: 2 -> 1, of which waited for: 2 -> 1; matrix products, arithmetic and copies ran while one was open for 5% -> 0% of each run, Pallas kernels for 0% -> 0%
where the time goes in v1:
time: 68.8 us; the launch traced here: 68.4 us
  blocking collectives  34.8 us (51%)
  waiting for transfers between devices  11.5 us (17%)
  Pallas kernels  11.2 us (16%)
  starting transfers between devices  10.2 us (15%)
  local copies, waits for them, and re-layouts  0.69 us (1%)
    all_to_all x1, blocking collectives, body(): lax.all_to_all(packed, 'grp', split_axis=0, concat_axis=0, tiled=True)  18.3 us
    all_to_all x1, blocking collectives, body(): lax.all_to_all(partial, 'blk', split_axis=0, concat_axis=0, tiled=True)  16.5 us
    all_to_all x1, waiting for transfers between devices, body(): lax.all_to_all(spread, 'blk', split_axis=0, concat_axis=0, tiled=True)  11.5 us
    all_to_all x1, starting transfers between devices, body(): lax.all_to_all(spread, 'blk', split_axis=0, concat_axis=0, tiled=True)  10.2 us
    pallas_call x1, Pallas kernels, body(): pl.pallas_call(attend_kernel, out_shape=jax.ShapeDtypeStruct((devices, RO...  6.14 us
    pallas_call x1, Pallas kernels, body(): pl.pallas_call(combine_kernel, out_shape=jax.ShapeDtypeStruct((TOK, HEADS...  1.98 us
    pallas_call x1, Pallas kernels, body(): pl.pallas_call(spread_kernel, out_shape=jax.ShapeDtypeStruct((devices, RO...  1.67 us
    pallas_call x1, Pallas kernels, body(): pl.pallas_call(pack_kernel, out_shape=jax.ShapeDtypeStruct((groups, feats...  1.41 us
  transfers between devices with their start and end apart: 1, of which 1 were waited for; matrix products, arithmetic and copies ran while one was open for 0% of the time, Pallas kernels for 0%

profile of v1, /device:TPU:8, one launch (start us, length us, event | category | flops | bytes accessed | tf_op | source)
XLA Modules:
  0.0 68.4 jit_solution(15664619650870329342)
XLA Ops:
  0.0 1.4 %pack.1 = bf16[16,16,128]{2,1,0:T(8,128)(2,1)} custom-call(bf16[16,192]{1,0:T(8,128)(2,1)} %bitcast.9), custom_call_target="tpu_custom_call" | custom-call | tf_op jit(solution)/shard_map/pack/pallas_call | solution.py:136
  1.4 18.3 %all_to_all.15 = bf16[16,16,128]{2,1,0:T(8,128)(2,1)} all-to-all(bf16[16,16,128]{2,1,0:T(8,128)(2,1)} %pack.1), channel_id=1, replica_groups=mesh['blk'=32,'grp'=16] {'grp'}, dimensions={0} | all-to-all | bytes 131072 | tf_op jit(solution)/shard_map/all_to_all | solution.py:143
  19.7 1.7 %spread.1 = bf16[32,24,128]{2,1,0:T(8,128)(2,1)} custom-call(bf16[256,128]{1,0:T(8,128)(2,1)} %bitcast.8), custom_call_target="tpu_custom_call" | custom-call | tf_op jit(solution)/shard_map/spread/pallas_call | solution.py:144
  21.4 10.2 %all-to-all-start.1 = ((bf16[32,24,128]{2,1,0:T(8,128)(2,1)}), bf16[32,24,128]{2,1,0:T(8,128)(2,1)S(1)}, u32[]{:S(2)}, u32[]{:S(2)}) async-start(bf16[32,24,128]{2,1,0:T(8,128)(2,1)} %spread.1), calls=%async_computation.1 | async-start | bytes 393216 | tf_op jit(solution)/shard_map/all_to_all | solution.py:151
  31.6 11.5 %all-to-all-done.1.q_ref = bf16[32,24,128]{2,1,0:T(8,128)(2,1)S(1)} async-done(((bf16[32,24,128]{2,1,0:T(8,128)(2,1)}), bf16[32,24,128]{2,1,0:T(8,128)(2,1)S(1)}, u32[]{:S(2)}, u32[]{:S(2)}) %all-to-all-start.1) | async-done | bytes 196640 | tf_op jit(solution)/shard_map/all_to_all | solution.py:151
  43.1 0.0 copy-start
  43.1 0.7 %copy-done = bf16[32,24,128]{2,1,0:T(8,128)(2,1)} copy-done((bf16[32,24,128]{2,1,0:T(8,128)(2,1)}, bf16[32,24,128]{2,1,0:T(8,128)(2,1)S(1)}, u32[]{:S(2)}) %copy-start) | copy-done | bytes 196632
  43.8 6.1 %attend.1 = bf16[32,32,128]{2,1,0:T(8,128)(2,1)} custom-call(s32[1]{0:T(128)} %bitcast.first_ref, s32[1,4]{1,0:T(1,128)} %len_ref.1, s32[4,128]{1,0:T(4,128)} %bitcast.10, bf16[32,24,128]{2,1,0:T(8,128)(2,1)} %copy-done, bf16[1024,1024]{1,0:T(8,128)(2,1)} %bitcast.6, bf16[1024,1024]{1,0:T(8,128)(2,1)} %bitcast.7), custom_call_target="tpu_custom_call" | custom-call | tf_op jit(solution)/shard_map/attend/pallas_call | solution.py:153
  49.9 16.5 %all_to_all.16.a_ref = bf16[32,32,128]{2,1,0:T(8,128)(2,1)} all-to-all(bf16[32,32,128]{2,1,0:T(8,128)(2,1)} %attend.1), channel_id=1, replica_groups=mesh['blk'=32,'grp'=16] {'blk'}, dimensions={0} | all-to-all | bytes 524288 | tf_op jit(solution)/shard_map/all_to_all | solution.py:167
  66.4 2.0 %combine.1 = bf16[12,256]{1,0:T(8,128)(2,1)} custom-call(bf16[32,32,128]{2,1,0:T(8,128)(2,1)} %all_to_all.16.a_ref), custom_call_target="tpu_custom_call" | custom-call | tf_op jit(solution)/shard_map/combine/pallas_call | solution.py:168
Async XLA Ops:
  21.4 21.7 %all-to-all-start.1 = ((bf16[32,24,128]{2,1,0:T(8,128)(2,1)}), bf16[32,24,128]{2,1,0:T(8,128)(2,1)S(1)}, u32[]{:S(2)}, u32[]{:S(2)}) async-start(bf16[32,24,128]{2,1,0:T(8,128)(2,1)} %spread.1), calls=%async_computation.1 | async-start | bytes 393216 | tf_op jit(solution)/shard_map/all_to_all | solution.py:151
  43.1 0.7 %copy-start = (bf16[32,24,128]{2,1,0:T(8,128)(2,1)}, bf16[32,24,128]{2,1,0:T(8,128)(2,1)S(1)}, u32[]{:S(2)}) copy-start(bf16[32,24,128]{2,1,0:T(8,128)(2,1)S(1)} %all-to-all-done.1.q_ref) | copy-start | bytes 589828

commit v2 on v1

--- a/solution.py
+++ b/solution.py
@@ -24,14 +24,30 @@
 EMPTY = -1e30
 
 VMEM = pl.BlockSpec(memory_space=pltpu.VMEM)
+HBM = pl.BlockSpec(memory_space=pltpu.HBM)
 SMEM = pl.BlockSpec(memory_space=pltpu.SMEM)
+
+
+PARAMS = pltpu.CompilerParams(vmem_limit_bytes=16 * 1024 * 1024)
+
+
+def in_hbm(array):
+    return pltpu.with_memory_space_constraint(array, pltpu.HBM)
 
 
 def iota(shape, dim):
     return lax.broadcasted_iota(jnp.int32, shape, dim)
 
 
-def pack_kernel(q_ref, out_ref):
+def pack_kernel(first_ref, len_hbm, table_hbm, q_hbm, out_ref, bias_ref, len_ref, table_ref, q_ref, sems):
+    copies = [
+        pltpu.make_async_copy(q_hbm, q_ref, sems.at[0]),
+        pltpu.make_async_copy(table_hbm, table_ref, sems.at[1]),
+        pltpu.make_async_copy(len_hbm, len_ref, sems.at[2]),
+    ]
+    for c in copies:
+        c.start()
+    copies[0].wait()
     groups, feats, _ = out_ref.shape
     q = q_ref[...].astype(jnp.float32)
     keep = iota((feats, LANES), 1) < TOK
@@ -40,6 +56,23 @@
         at = g * TOK
         shifted = wide if at == 0 else pltpu.roll(wide, 2 * LANES - at, 1)
         out_ref[g] = jnp.where(keep, shifted[:, :LANES], 0.0).astype(out_ref.dtype)
+    copies[1].wait()
+    copies[2].wait()
+    lane4 = iota((SEQS, LANES), 1)
+    sub4 = iota((SEQS, LANES), 0)
+    lens = jnp.zeros((SEQS, LANES), jnp.int32)
+    for q in range(SEQS):
+        lens = jnp.where(sub4 == q, len_ref[0, q], lens)
+    local = jnp.where(lane4 < lens, table_ref[...] - first_ref[0], -1)
+    row = iota((ROWS, LANES), 0)
+    seq = jnp.where(row >= TOK, row - TOK, row) // STEPS
+    for s in range(SLOTS):
+        hit = jnp.max((local == s).astype(jnp.float32), axis=1, keepdims=True)
+        off = jnp.broadcast_to(jnp.where(hit > 0.0, 0.0, EMPTY), (SEQS, LANES))
+        b = jnp.broadcast_to(off[0:1], (ROWS, LANES))
+        for q in range(1, SEQS):
+            b = jnp.where(seq == q, off[q : q + 1], b)
+        bias_ref[:, s * BLOCK : (s + 1) * BLOCK] = b
 
 
 def spread_kernel(a_ref, out_ref):
@@ -54,25 +87,19 @@
         out_ref[b] = rows
 
 
-def attend_kernel(first_ref, len_ref, table_ref, q_ref, k_ref, v_ref, out_ref):
-    lane4 = iota((SEQS, LANES), 1)
-    sub4 = iota((SEQS, LANES), 0)
-    lens = jnp.zeros((SEQS, LANES), jnp.int32)
-    for q in range(SEQS):
-        lens = jnp.where(sub4 == q, len_ref[0, q], lens)
-    local = jnp.where(lane4 < lens, table_ref[...] - first_ref[0], -1)
-    row = iota((ROWS, LANES), 0)
-    seq = jnp.where(row >= TOK, row - TOK, row) // STEPS
-    bias = []
-    for s in range(SLOTS):
-        hit = jnp.max((local == s).astype(jnp.float32), axis=1, keepdims=True)
-        off = jnp.broadcast_to(jnp.where(hit > 0.0, 0.0, EMPTY), (SEQS, LANES))
-        b = jnp.broadcast_to(off[0:1], (ROWS, LANES))
-        for q in range(1, SEQS):
-            b = jnp.where(seq == q, off[q : q + 1], b)
-        bias.append(b)
-    bias = jnp.concatenate(bias, axis=1)
-    bias = jnp.concatenate([bias] * SLICES, axis=0)
+def attend_kernel(bias_ref, q_ref, k_hbm, v_hbm, out_ref, k_ref, v_ref, sems):
+    def load(k):
+        cols = pl.ds(k * DH, DH)
+        return (
+            pltpu.make_async_copy(k_hbm.at[:, cols], k_ref.at[:, cols], sems.at[0, k]),
+            pltpu.make_async_copy(v_hbm.at[:, cols], v_ref.at[:, cols], sems.at[1, k]),
+        )
+
+    loads = [load(k) for k in range(KVH)]
+    for pair in loads:
+        for c in pair:
+            c.start()
+    bias = jnp.concatenate([bias_ref[...]] * SLICES, axis=0)
 
     rows = SLICES * ROWS
     lane = iota((rows, LANES), 1)
@@ -81,11 +108,13 @@
     nn = (((1,), (0,)), ((), ()))
     for k in range(KVH):
         cols = slice(k * DH, (k + 1) * DH)
+        loads[k][0].wait()
         qk = q_ref[k * SLICES : (k + 1) * SLICES].reshape(rows, DH)
         s = lax.dot_general(qk, k_ref[:, cols], nt, preferred_element_type=jnp.float32) + bias
         top = jnp.max(s, axis=1, keepdims=True)
         p = jnp.exp2((s - top) * SCALE).astype(jnp.bfloat16)
         total = jnp.sum(p.astype(jnp.float32), axis=1, keepdims=True)
+        loads[k][1].wait()
         o = lax.dot_general(p, v_ref[:, cols], nn, preferred_element_type=jnp.float32)
         o = (o / total).astype(out_ref.dtype)
         lse = jnp.where(lane == k, top * SCALE + jnp.log2(total), lse)
@@ -133,43 +162,55 @@
     groups = lax.axis_size("grp")
     devices = lax.axis_size("blk")
     feats = queries.shape[1]
-    packed = pl.pallas_call(
+    first = (lax.axis_index("blk") * SLOTS).astype(jnp.int32).reshape(1)
+    packed, bias = pl.pallas_call(
         pack_kernel,
-        out_shape=jax.ShapeDtypeStruct((groups, feats, LANES), bf16),
-        in_specs=[VMEM],
-        out_specs=VMEM,
+        out_shape=(
+            jax.ShapeDtypeStruct((groups, feats, LANES), bf16),
+            jax.ShapeDtypeStruct((ROWS, SLOTS * BLOCK), jnp.float32),
+        ),
+        in_specs=[SMEM, HBM, HBM, HBM],
+        out_specs=(VMEM, VMEM),
+        scratch_shapes=[
+            pltpu.SMEM(lengths.shape, jnp.int32),
+            pltpu.VMEM(block_table.shape[1:], jnp.int32),
+            pltpu.VMEM((feats, queries.shape[0]), bf16),
+            pltpu.SemaphoreType.DMA((3,)),
+        ],
+        compiler_params=PARAMS,
         name="pack",
-    )(queries.T)
+    )(first, in_hbm(lengths), in_hbm(block_table[0]), in_hbm(queries.T))
     arrived = lax.all_to_all(packed, "grp", split_axis=0, concat_axis=0, tiled=True)
     spread = pl.pallas_call(
         spread_kernel,
         out_shape=jax.ShapeDtypeStruct((devices, ROWS, LANES), bf16),
         in_specs=[VMEM],
         out_specs=VMEM,
+        compiler_params=PARAMS,
         name="spread",
     )(arrived.reshape(groups * feats, LANES))
     query_all = lax.all_to_all(spread, "blk", split_axis=0, concat_axis=0, tiled=True)
-    first = (lax.axis_index("blk") * SLOTS).astype(jnp.int32).reshape(1)
+    pool = (SLOTS * BLOCK, KVH * DH)
     partial = pl.pallas_call(
         attend_kernel,
         out_shape=jax.ShapeDtypeStruct((devices, ROWS + 8, LANES), bf16),
-        in_specs=[SMEM, SMEM, VMEM, VMEM, VMEM, VMEM],
+        in_specs=[VMEM, VMEM, HBM, HBM],
         out_specs=VMEM,
+        scratch_shapes=[
+            pltpu.VMEM(pool, bf16),
+            pltpu.VMEM(pool, bf16),
+            pltpu.SemaphoreType.DMA((2, KVH)),
+        ],
+        compiler_params=PARAMS,
         name="attend",
-    )(
-        first,
-        lengths,
-        block_table[0],
-        query_all,
-        key_pool.reshape(SLOTS * BLOCK, KVH * DH),
-        value_pool.reshape(SLOTS * BLOCK, KVH * DH),
-    )
+    )(bias, query_all, in_hbm(key_pool.reshape(pool)), in_hbm(value_pool.reshape(pool)))
     collected = lax.all_to_all(partial, "blk", split_axis=0, concat_axis=0, tiled=True)
     return pl.pallas_call(
         combine_kernel,
         out_shape=jax.ShapeDtypeStruct((TOK, HEADS * DH), bf16),
         in_specs=[VMEM],
         out_specs=VMEM,
+        compiler_params=PARAMS,
         name="combine",
     )(collected)
 

time: 68.8 us -> 64.5 us (0.938)
  blocking collectives: 34.8 us -> 55.7 us
  waiting for transfers between devices: 11.5 us -> 0 us
  starting transfers between devices: 10.2 us -> 0 us
  Pallas kernels: 11.2 us -> 8.54 us
  local copies, waits for them, and re-layouts: 0.69 us -> 0 us
    all_to_all x0 -> x1, blocking collectives: none -> 21.5 us  [body(): lax.all_to_all(spread, 'blk', split_axis=0, concat_axis=0, tiled=True)]
    all_to_all x1 -> x0, waiting for transfers between devices: 11.5 us -> none  [body(): lax.all_to_all(spread, 'blk', split_axis=0, concat_axis=0, tiled=True)]
    all_to_all x1 -> x0, starting transfers between devices: 10.2 us -> none  [body(): lax.all_to_all(spread, 'blk', split_axis=0, concat_axis=0, tiled=True)]
    pallas_call x1, Pallas kernels: 1.67 us -> 0.16 us  [body(): pl.pallas_call(spread_kernel, out_shape=jax.ShapeDtypeStruct((devices, RO...]
    pallas_call x1, Pallas kernels: 1.98 us -> 1.04 us  [body(): pl.pallas_call(combine_kernel, out_shape=jax.ShapeDtypeStruct((TOK, HEADS...]
  transfers between devices with their start and end apart: 1 -> 0, of which waited for: 1 -> 0; matrix products, arithmetic and copies ran while one was open for 0% -> 0% of each run, Pallas kernels for 0% -> 0%
where the time goes in v2:
time: 64.5 us; the launch traced here: 64.2 us
  blocking collectives  55.7 us (86%)
  Pallas kernels  8.54 us (13%)
    all_to_all x1, blocking collectives, body(): lax.all_to_all(spread, 'blk', split_axis=0, concat_axis=0, tiled=True)  21.5 us
    all_to_all x1, blocking collectives, body(): lax.all_to_all(packed, 'grp', split_axis=0, concat_axis=0, tiled=True)  18 us
    all_to_all x1, blocking collectives, body(): lax.all_to_all(partial, 'blk', split_axis=0, concat_axis=0, tiled=True)  16.1 us
    pallas_call x1, Pallas kernels, body(): pl.pallas_call(attend_kernel, out_shape=jax.ShapeDtypeStruct((devices, RO...  6.41 us

profile of v2, /device:TPU:8, one launch (start us, length us, event | category | flops | bytes accessed | tf_op | source)
XLA Modules:
  0.0 64.2 jit_solution(7763797482665480803)
XLA Ops:
  0.0 0.9 %pack.1 = (bf16[16,16,128]{2,1,0:T(8,128)(2,1)S(1)}, f32[24,1024]{1,0:T(8,128)S(1)}) custom-call(s32[1]{0:T(128)} %bitcast.first_ref, s32[1,4]{1,0:T(1,128)} %len_hbm.1, s32[4,128]{1,0:T(4,128)} %bitcast.10, bf16[16,192]{1,0:T(8,128)(2,1)} %bitcast.9), custom_call_target="tpu_custom_call" | custom-call | tf_op jit(solution)/shard_map/pack/pallas_call | solution.py:166
  0.9 18.0 %all_to_all.15 = bf16[16,16,128]{2,1,0:T(8,128)(2,1)S(1)} all-to-all(bf16[16,16,128]{2,1,0:T(8,128)(2,1)S(1)} %get-tuple-element.8), channel_id=1, replica_groups=mesh['blk'=32,'grp'=16] {'grp'}, dimensions={0} | all-to-all | bytes 131072 | tf_op jit(solution)/shard_map/all_to_all | solution.py:183
  19.0 0.2 spread.1
  19.1 21.5 %all_to_all.16.q_ref = bf16[32,24,128]{2,1,0:T(8,128)(2,1)S(1)} all-to-all(bf16[32,24,128]{2,1,0:T(8,128)(2,1)S(1)} %spread.1), channel_id=1, replica_groups=mesh['blk'=32,'grp'=16] {'blk'}, dimensions={0} | all-to-all | bytes 393216 | tf_op jit(solution)/shard_map/all_to_all | solution.py:192
  40.6 6.4 %attend.1 = bf16[32,32,128]{2,1,0:T(8,128)(2,1)S(1)} custom-call(f32[24,1024]{1,0:T(8,128)S(1)} %get-tuple-element.7.bias_ref, bf16[32,24,128]{2,1,0:T(8,128)(2,1)S(1)} %all_to_all.16.q_ref, bf16[1024,1024]{1,0:T(8,128)(2,1)} %bitcast.7, bf16[1024,1024]{1,0:T(8,128)(2,1)} %bitcast.8), custom_call_target="tpu_custom_call" | custom-call | tf_op jit(solution)/shard_map/attend/pallas_call | solution.py:194
  47.1 16.1 %all_to_all.17.a_ref = bf16[32,32,128]{2,1,0:T(8,128)(2,1)S(1)} all-to-all(bf16[32,32,128]{2,1,0:T(8,128)(2,1)S(1)} %attend.1), channel_id=1, replica_groups=mesh['blk'=32,'grp'=16] {'blk'}, dimensions={0} | all-to-all | bytes 524288 | tf_op jit(solution)/shard_map/all_to_all | solution.py:207
  63.2 1.0 %combine.1 = bf16[12,256]{1,0:T(8,128)(2,1)} custom-call(bf16[32,32,128]{2,1,0:T(8,128)(2,1)S(1)} %all_to_all.17.a_ref), custom_call_target="tpu_custom_call" | custom-call | tf_op jit(solution)/shard_map/combine/pallas_call | solution.py:208

commit v3 on v2

--- a/solution.py
+++ b/solution.py
@@ -18,6 +18,8 @@
 SLICES = 4
 SLOTS = 8
 BLOCK = 128
+FETCHES = 8
+EARLY = 4
 LANES = 128
 SCALE = math.log2(math.e) / math.sqrt(DH)
 LN2 = math.log(2.0)
@@ -87,18 +89,31 @@
         out_ref[b] = rows
 
 
-def attend_kernel(bias_ref, q_ref, k_hbm, v_hbm, out_ref, k_ref, v_ref, sems):
-    def load(k):
-        cols = pl.ds(k * DH, DH)
-        return (
-            pltpu.make_async_copy(k_hbm.at[:, cols], k_ref.at[:, cols], sems.at[0, k]),
-            pltpu.make_async_copy(v_hbm.at[:, cols], v_ref.at[:, cols], sems.at[1, k]),
+def fetch_kernel(k_hbm, v_hbm, k_ref, v_ref, sems):
+    rows = k_ref.shape[0] // FETCHES
+    copies = []
+    for i in range(FETCHES):
+        at = pl.ds(i * rows, rows)
+        copies.append(pltpu.make_async_copy(k_hbm.at[at], k_ref.at[at], sems.at[0, i]))
+        copies.append(
+            pltpu.make_async_copy(v_hbm.at[at, pl.ds(0, EARLY * DH)], v_ref.at[at], sems.at[1, i])
         )
-
-    loads = [load(k) for k in range(KVH)]
-    for pair in loads:
-        for c in pair:
-            c.start()
+    for c in copies:
+        c.start()
+    for c in copies:
+        c.wait()
+
+
+def attend_kernel(bias_ref, q_ref, k_ref, v_ref, v_hbm, out_ref, late_ref, sems):
+    late = []
+    for k in range(EARLY, KVH):
+        to = pl.ds((k - EARLY) * DH, DH)
+        late.append(
+            pltpu.make_async_copy(
+                v_hbm.at[:, pl.ds(k * DH, DH)], late_ref.at[:, to], sems.at[k - EARLY]
+            )
+        )
+        late[-1].start()
     bias = jnp.concatenate([bias_ref[...]] * SLICES, axis=0)
 
     rows = SLICES * ROWS
@@ -108,14 +123,17 @@
     nn = (((1,), (0,)), ((), ()))
     for k in range(KVH):
         cols = slice(k * DH, (k + 1) * DH)
-        loads[k][0].wait()
         qk = q_ref[k * SLICES : (k + 1) * SLICES].reshape(rows, DH)
         s = lax.dot_general(qk, k_ref[:, cols], nt, preferred_element_type=jnp.float32) + bias
         top = jnp.max(s, axis=1, keepdims=True)
         p = jnp.exp2((s - top) * SCALE).astype(jnp.bfloat16)
         total = jnp.sum(p.astype(jnp.float32), axis=1, keepdims=True)
-        loads[k][1].wait()
-        o = lax.dot_general(p, v_ref[:, cols], nn, preferred_element_type=jnp.float32)
+        if k < EARLY:
+            v = v_ref[:, cols]
+        else:
+            late[k - EARLY].wait()
+            v = late_ref[:, (k - EARLY) * DH : (k - EARLY + 1) * DH]
+        o = lax.dot_general(p, v, nn, preferred_element_type=jnp.float32)
         o = (o / total).astype(out_ref.dtype)
         lse = jnp.where(lane == k, top * SCALE + jnp.log2(total), lse)
         out_ref[k * SLICES : (k + 1) * SLICES, :ROWS, :] = o.reshape(SLICES, ROWS, DH)
@@ -189,21 +207,32 @@
         compiler_params=PARAMS,
         name="spread",
     )(arrived.reshape(groups * feats, LANES))
+    pool = (SLOTS * BLOCK, KVH * DH)
+    k_hbm = in_hbm(key_pool.reshape(pool))
+    v_hbm = in_hbm(value_pool.reshape(pool))
+    keys, values = pl.pallas_call(
+        fetch_kernel,
+        out_shape=(pltpu.VMEM(pool, bf16), pltpu.VMEM((pool[0], EARLY * DH), bf16)),
+        in_specs=[HBM, HBM],
+        out_specs=(VMEM, VMEM),
+        scratch_shapes=[pltpu.SemaphoreType.DMA((2, FETCHES))],
+        compiler_params=PARAMS,
+        cost_estimate=pl.CostEstimate(flops=10**9, bytes_accessed=8 * 2**20, transcendentals=0),
+        name="fetch",
+    )(k_hbm, v_hbm)
     query_all = lax.all_to_all(spread, "blk", split_axis=0, concat_axis=0, tiled=True)
-    pool = (SLOTS * BLOCK, KVH * DH)
     partial = pl.pallas_call(
         attend_kernel,
         out_shape=jax.ShapeDtypeStruct((devices, ROWS + 8, LANES), bf16),
-        in_specs=[VMEM, VMEM, HBM, HBM],
+        in_specs=[VMEM, VMEM, VMEM, VMEM, HBM],
         out_specs=VMEM,
         scratch_shapes=[
-            pltpu.VMEM(pool, bf16),
-            pltpu.VMEM(pool, bf16),
-            pltpu.SemaphoreType.DMA((2, KVH)),
+            pltpu.VMEM((SLOTS * BLOCK, (KVH - EARLY) * DH), bf16),
+            pltpu.SemaphoreType.DMA((KVH - EARLY,)),
         ],
         compiler_params=PARAMS,
         name="attend",
-    )(bias, query_all, in_hbm(key_pool.reshape(pool)), in_hbm(value_pool.reshape(pool)))
+    )(bias, query_all, keys, values, v_hbm)
     collected = lax.all_to_all(partial, "blk", split_axis=0, concat_axis=0, tiled=True)
     return pl.pallas_call(
         combine_kernel,

time: 64.5 us -> 62.9 us (0.975)
  blocking collectives: 55.7 us -> 34.2 us
  starting transfers between devices: 0 us -> 10.2 us
  waiting for transfers between devices: 0 us -> 9.56 us
    all_to_all x1 -> x0, blocking collectives: 21.5 us -> none  [body(): lax.all_to_all(spread, 'blk', split_axis=0, concat_axis=0, tiled=True)]
    all_to_all x0 -> x1, starting transfers between devices: none -> 10.2 us  [body(): lax.all_to_all(spread, 'blk', split_axis=0, concat_axis=0, tiled=True)]
    all_to_all x0 -> x1, waiting for transfers between devices: none -> 9.56 us  [body(): lax.all_to_all(spread, 'blk', split_axis=0, concat_axis=0, tiled=True)]
    pallas_call x1, Pallas kernels: 6.41 us -> 3.82 us  [body(): pl.pallas_call(attend_kernel, out_shape=jax.ShapeDtypeStruct((devices, RO...]
    pallas_call x0 -> x1, Pallas kernels: none -> 1.98 us  [body(): pl.pallas_call(fetch_kernel, out_shape=(pltpu.VMEM(pool, bf16), pltpu.VME...]
    pallas_call x1, Pallas kernels: 0.16 us -> 0.83 us  [body(): pl.pallas_call(spread_kernel, out_shape=jax.ShapeDtypeStruct((devices, RO...]
  transfers between devices with their start and end apart: 0 -> 1, of which waited for: 0 -> 1; matrix products, arithmetic and copies ran while one was open for 0% -> 0% of each run, Pallas kernels for 0% -> 3%
where the time goes in v3:
time: 62.9 us; the launch traced here: 62.5 us
  blocking collectives  34.2 us (54%)
  starting transfers between devices  10.2 us (16%)
  waiting for transfers between devices  9.56 us (15%)
  Pallas kernels  8.61 us (14%)
    all_to_all x1, blocking collectives, body(): lax.all_to_all(packed, 'grp', split_axis=0, concat_axis=0, tiled=True)  18 us
    all_to_all x1, blocking collectives, body(): lax.all_to_all(partial, 'blk', split_axis=0, concat_axis=0, tiled=True)  16.1 us
    all_to_all x1, starting transfers between devices, body(): lax.all_to_all(spread, 'blk', split_axis=0, concat_axis=0, tiled=True)  10.2 us
    all_to_all x1, waiting for transfers between devices, body(): lax.all_to_all(spread, 'blk', split_axis=0, concat_axis=0, tiled=True)  9.56 us
    pallas_call x1, Pallas kernels, body(): pl.pallas_call(attend_kernel, out_shape=jax.ShapeDtypeStruct((devices, RO...  3.82 us
    pallas_call x1, Pallas kernels, body(): pl.pallas_call(fetch_kernel, out_shape=(pltpu.VMEM(pool, bf16), pltpu.VME...  1.98 us
  transfers between devices with their start and end apart: 1, of which 1 were waited for; matrix products, arithmetic and copies ran while one was open for 0% of the time, Pallas kernels for 3%

profile of v3, /device:TPU:8, one launch (start us, length us, event | category | flops | bytes accessed | tf_op | source)
XLA Modules:
  0.0 62.5 jit_solution(5379457647049606768)
XLA Ops:
  0.0 0.9 %pack.1 = (bf16[16,16,128]{2,1,0:T(8,128)(2,1)S(1)}, f32[24,1024]{1,0:T(8,128)S(1)}) custom-call(s32[1]{0:T(128)} %bitcast.first_ref, s32[1,4]{1,0:T(1,128)} %len_hbm.1, s32[4,128]{1,0:T(4,128)} %bitcast.11, bf16[16,192]{1,0:T(8,128)(2,1)} %bitcast.10), custom_call_target="tpu_custom_call" | custom-call | tf_op jit(solution)/shard_map/pack/pallas_call | solution.py:184
  0.9 18.0 %all_to_all.15 = bf16[16,16,128]{2,1,0:T(8,128)(2,1)S(1)} all-to-all(bf16[16,16,128]{2,1,0:T(8,128)(2,1)S(1)} %get-tuple-element.10), channel_id=1, replica_groups=mesh['blk'=32,'grp'=16] {'grp'}, dimensions={0} | all-to-all | bytes 131072 | tf_op jit(solution)/shard_map/all_to_all | solution.py:201
  19.0 0.8 %spread.1 = bf16[32,24,128]{2,1,0:T(8,128)(2,1)} custom-call(bf16[256,128]{1,0:T(8,128)(2,1)S(1)} %bitcast.6), custom_call_target="tpu_custom_call" | custom-call | tf_op jit(solution)/shard_map/spread/pallas_call | solution.py:202
  19.8 10.2 %all-to-all-start.1 = ((bf16[32,24,128]{2,1,0:T(8,128)(2,1)}), bf16[32,24,128]{2,1,0:T(8,128)(2,1)S(1)}, u32[]{:S(2)}, u32[]{:S(2)}) async-start(bf16[32,24,128]{2,1,0:T(8,128)(2,1)} %spread.1), calls=%async_computation.1 | async-start | bytes 393216 | tf_op jit(solution)/shard_map/all_to_all | solution.py:223
  30.0 2.0 %fetch.1 = (bf16[1024,1024]{1,0:T(8,128)(2,1)S(1)}, bf16[1024,512]{1,0:T(8,128)(2,1)S(1)}) custom-call(bf16[1024,1024]{1,0:T(8,128)(2,1)} %bitcast.9, bf16[1024,1024]{1,0:T(8,128)(2,1)} %bitcast.7), custom_call_target="tpu_custom_call" | custom-call | flops 1000000000 | bytes 8388608 | tf_op jit(solution)/shard_map/fetch/pallas_call | solution.py:213
  32.0 9.6 %all-to-all-done.1.q_ref = bf16[32,24,128]{2,1,0:T(8,128)(2,1)S(1)} async-done(((bf16[32,24,128]{2,1,0:T(8,128)(2,1)}), bf16[32,24,128]{2,1,0:T(8,128)(2,1)S(1)}, u32[]{:S(2)}, u32[]{:S(2)}) %all-to-all-start.1) | async-done | bytes 196640 | tf_op jit(solution)/shard_map/all_to_all | solution.py:223
  41.5 3.8 %attend.1 = bf16[32,32,128]{2,1,0:T(8,128)(2,1)S(1)} custom-call(f32[24,1024]{1,0:T(8,128)S(1)} %get-tuple-element.9.bias_ref, bf16[32,24,128]{2,1,0:T(8,128)(2,1)S(1)} %all-to-all-done.1.q_ref, bf16[1024,1024]{1,0:T(8,128)(2,1)S(1)} %get-tuple-element.11.k_ref, bf16[1024,512]{1,0:T(8,128)(2,1)S(1)} %get-tuple-element.12.v_ref, bf16[1024,1024]{1,0:T(8,128)(2,1)} %bitcast.8), custom_call_target="tpu_custom_call" | custom-call | tf_op jit(solution)/shard_map/attend/pallas_call | solution.py:224
  45.3 16.1 %all_to_all.16.a_ref = bf16[32,32,128]{2,1,0:T(8,128)(2,1)S(1)} all-to-all(bf16[32,32,128]{2,1,0:T(8,128)(2,1)S(1)} %attend.1), channel_id=1, replica_groups=mesh['blk'=32,'grp'=16] {'blk'}, dimensions={0} | all-to-all | bytes 524288 | tf_op jit(solution)/shard_map/all_to_all | solution.py:236
  61.5 1.0 %combine.1 = bf16[12,256]{1,0:T(8,128)(2,1)} custom-call(bf16[32,32,128]{2,1,0:T(8,128)(2,1)S(1)} %all_to_all.16.a_ref), custom_call_target="tpu_custom_call" | custom-call | tf_op jit(solution)/shard_map/combine/pallas_call | solution.py:237
Async XLA Ops:
  19.8 21.7 %all-to-all-start.1 = ((bf16[32,24,128]{2,1,0:T(8,128)(2,1)}), bf16[32,24,128]{2,1,0:T(8,128)(2,1)S(1)}, u32[]{:S(2)}, u32[]{:S(2)}) async-start(bf16[32,24,128]{2,1,0:T(8,128)(2,1)} %spread.1), calls=%async_computation.1 | async-start | bytes 393216 | tf_op jit(solution)/shard_map/all_to_all | solution.py:223

commit v4 on v3

v4 whole, which is shorter than its diff:
```python
import math

import jax
import jax.numpy as jnp
from jax import lax
from jax.experimental import pallas as pl
from jax.experimental.pallas import tpu as pltpu
from jax.sharding import PartitionSpec as P

HQ = 64
KVH = 8
DH = 128
STEPS = 3
SEQS = 4
TOK = SEQS * STEPS
HEADS = 2
ROWS = HEADS * TOK
PART = HEADS * STEPS
SLICES = 4
SLOTS = 8
GAP = 32
LANES_A_SLOT = 16
BLOCK = 128
FETCHES = 8
EARLY = 4
LANES = 128
SCALE = math.log2(math.e) / math.sqrt(DH)
LN2 = math.log(2.0)
EMPTY = -1e30

VMEM = pl.BlockSpec(memory_space=pltpu.VMEM)
HBM = pl.BlockSpec(memory_space=pltpu.HBM)
SMEM = pl.BlockSpec(memory_space=pltpu.SMEM)


PARAMS = pltpu.CompilerParams(vmem_limit_bytes=16 * 1024 * 1024)


def in_hbm(array):
    return pltpu.with_memory_space_constraint(array, pltpu.HBM)


def iota(shape, dim):
    return lax.broadcasted_iota(jnp.int32, shape, dim)


def pack_kernel(q_ref, out_ref):
    groups, feats, _ = out_ref.shape
    q = q_ref[...].astype(jnp.float32)
    keep = iota((feats, LANES), 1) < TOK
    wide = jnp.concatenate([q, jnp.zeros((feats, 2 * LANES - q.shape[1]), jnp.float32)], axis=1)
    for g in range(groups):
        at = g * TOK
        shifted = wide if at == 0 else pltpu.roll(wide, 2 * LANES - at, 1)
        out_ref[g] = jnp.where(keep, shifted[:, :LANES], 0.0).astype(out_ref.dtype)


def spread_kernel(a_ref, out_ref):
    row = iota((ROWS, LANES), 0)
    tok = jnp.where(row >= TOK, row - TOK, row)
    pick = (tok == iota((ROWS, LANES), 1)).astype(jnp.bfloat16)
    nt = (((1,), (1,)), ((), ()))
    first = lax.dot_general(pick, a_ref[:LANES, :], nt, preferred_element_type=jnp.float32)
    second = lax.dot_general(pick, a_ref[LANES:, :], nt, preferred_element_type=jnp.float32)
    rows = jnp.where(row < TOK, first, second).astype(out_ref.dtype)
    for b in range(out_ref.shape[0]):
        out_ref[b] = rows


def place(q, r):
    slice_, rest = r // PART, r % PART
    return slice_ * ROWS + (rest // STEPS) * TOK + q * STEPS + rest % STEPS


def fetch_kernel(
    first_ref, len_hbm, table_hbm, k_hbm, v_hbm,
    k_ref, v_ref, gather_ref, scatter_ref, own_ref, owner_ref,
    len_ref, table_ref, sems, small,
):
    rows = k_ref.shape[0] // FETCHES
    copies = []
    for i in range(FETCHES):
        at = pl.ds(i * rows, rows)
        copies.append(pltpu.make_async_copy(k_hbm.at[at], k_ref.at[at], sems.at[0, i]))
        copies.append(
            pltpu.make_async_copy(v_hbm.at[at, pl.ds(0, EARLY * DH)], v_ref.at[at], sems.at[1, i])
        )
    facts = [
        pltpu.make_async_copy(table_hbm, table_ref, small.at[0]),
        pltpu.make_async_copy(len_hbm, len_ref, small.at[1]),
    ]
    for c in facts + copies:
        c.start()
    for c in facts:
        c.wait()
    lane4 = iota((SEQS, LANES), 1)
    sub4 = iota((SEQS, LANES), 0)
    lens = jnp.zeros((SEQS, LANES), jnp.int32)
    for q in range(SEQS):
        lens = jnp.where(sub4 == q, len_ref[0, q], lens)
    local = jnp.where(lane4 < lens, table_ref[...] - first_ref[0], -1)
    r = iota((GAP, LANES), 0)
    c = iota((GAP, LANES), 1)
    lane8 = iota((8, LANES), 1) // LANES_A_SLOT
    owner = jnp.full((8, LANES), -1, jnp.int32)
    for s in range(SLOTS):
        hit = jnp.max((local == s).astype(jnp.float32), axis=1, keepdims=True)
        own_ref[s * SEQS : (s + 1) * SEQS, :] = jnp.broadcast_to(hit, (SEQS, LANES))
        q = jnp.max(jnp.where(hit > 0.0, sub4[:, :1], -1).astype(jnp.float32), axis=0, keepdims=True)
        q = jnp.broadcast_to(q.astype(jnp.int32), (8, LANES))
        owner = jnp.where(lane8 == s, q, owner)
        q = jnp.broadcast_to(q[:1], (GAP, LANES))
        pick = (c == place(q, r)) & (r < SLICES * PART) & (q >= 0)
        gather_ref[s * GAP : (s + 1) * GAP, :] = pick.astype(jnp.float32).astype(jnp.bfloat16)
    owner_ref[...] = owner
    n = SEQS * SLICES * PART
    to = iota((n, LANES), 0)
    row = iota((n, LANES), 1)
    pick = (to == place(row // (SLICES * PART), row % (SLICES * PART))) & (row < n)
    scatter_ref[...] = pick.astype(jnp.float32).astype(jnp.bfloat16)
    for c in copies:
        c.wait()


def attend_kernel(
    gather_ref, scatter_ref, own_ref, owner_ref, q_ref, k_ref, v_ref, v_hbm,
    out_ref, late_ref, s_ref, sems,
):
    late = []
    for k in range(EARLY, KVH):
        to = pl.ds((k - EARLY) * DH, DH)
        late.append(
            pltpu.make_async_copy(
                v_hbm.at[:, pl.ds(k * DH, DH)], late_ref.at[:, to], sems.at[k - EARLY]
            )
        )
        late[-1].start()
    one = SLICES * PART
    rows = SEQS * one
    nt = (((1,), (1,)), ((), ()))
    nn = (((1,), (0,)), ((), ()))
    gather = gather_ref[:, :rows]
    scatter = scatter_ref[:, :rows]
    lane = iota((one, LANES), 1)

    top = jnp.full((one, LANES), EMPTY, jnp.float32)
    for k in range(KVH):
        cols = slice(k * DH, (k + 1) * DH)
        qk = q_ref[k * SLICES : (k + 1) * SLICES].reshape(rows, DH)
        qs = lax.dot_general(gather, qk, nn, preferred_element_type=jnp.float32)
        qs = qs.astype(jnp.bfloat16)
        for s in range(SLOTS):
            scores = lax.dot_general(
                qs[s * GAP : (s + 1) * GAP],
                k_ref[s * BLOCK : (s + 1) * BLOCK, cols],
                nt,
                preferred_element_type=jnp.float32,
            )[:one]
            s_ref[k * SLOTS + s] = scores
            most = jnp.max(scores, axis=1, keepdims=True)
            top = jnp.where(lane == s * LANES_A_SLOT + k, most, top)

    owner = jnp.concatenate([owner_ref[...]] * (one // 8), axis=0)
    slot_top = top
    seq_top = []
    for q in range(SEQS):
        t = jnp.where(owner == q, top, EMPTY)
        for shift in (16, 32, 64):
            t = jnp.maximum(t, pltpu.roll(t, shift, 1))
        seq_top.append(t)
        slot_top = jnp.where(owner == q, t, slot_top)

    wide = iota((rows, LANES), 1)
    totals = jnp.zeros((rows, LANES), jnp.float32)
    for k in range(KVH):
        cols = slice(k * DH, (k + 1) * DH)
        parts = [[] for _ in range(SEQS)]
        for s in range(SLOTS):
            at = s * LANES_A_SLOT + k
            p = jnp.exp2((s_ref[k * SLOTS + s] - slot_top[:, at : at + 1]) * SCALE)
            for q in range(SEQS):
                parts[q].append(p * own_ref[s * SEQS + q : s * SEQS + q + 1, :])
        sums = jnp.concatenate([sum(x[1:], x[0]) for x in parts], axis=0)
        total = jnp.sum(sums, axis=1, keepdims=True)
        p = jnp.concatenate(
            [
                jnp.concatenate([parts[q][s] for q in range(SEQS)], axis=0).astype(jnp.bfloat16)
                for s in range(SLOTS)
            ],
            axis=1,
        )
        if k < EARLY:
            v = v_ref[:, cols]
        else:
            late[k - EARLY].wait()
            v = late_ref[:, (k - EARLY) * DH : (k - EARLY + 1) * DH]
        o = lax.dot_general(p, v, nn, preferred_element_type=jnp.float32)
        o = jnp.where(total > 0.0, o / jnp.where(total > 0.0, total, 1.0), 0.0)
        o = lax.dot_general(
            scatter, o.astype(jnp.bfloat16), nn, preferred_element_type=jnp.float32
        ).astype(out_ref.dtype)
        out_ref[k * SLICES : (k + 1) * SLICES, :ROWS, :] = o.reshape(SLICES, ROWS, DH)
        totals = jnp.where(wide == k, total, totals)

    some = totals > 0.0
    lse = jnp.concatenate(seq_top, axis=0) * SCALE
    lse = jnp.where(some, lse + jnp.log2(jnp.where(some, totals, 1.0)), EMPTY)
    lse = jnp.where(wide < KVH, lse, 0.0)
    high = lse.astype(jnp.bfloat16).astype(jnp.float32)
    rest = lse - high
    mid = rest.astype(jnp.bfloat16).astype(jnp.float32)
    low = rest - mid
    pieces = high + pltpu.roll(mid, KVH, 1) + pltpu.roll(low, 2 * KVH, 1)
    pieces = lax.dot_general(
        scatter, pieces.astype(jnp.bfloat16), nn, preferred_element_type=jnp.float32
    )
    square = jnp.concatenate([pieces, jnp.zeros((LANES - rows, LANES), jnp.float32)], axis=0)
    flat = jnp.transpose(square)
    lane8 = iota((KVH, LANES), 1)
    for j in range(SLICES):
        line = jnp.zeros((KVH, LANES), jnp.float32)
        for i in range(3):
            shift = (32 * i - j * ROWS) % LANES
            part = flat[i * KVH : (i + 1) * KVH]
            part = part if shift == 0 else pltpu.roll(part, shift, 1)
            line = jnp.where((lane8 >= 32 * i) & (lane8 < 32 * i + ROWS), part, line)
        for k in range(KVH):
            tile = jnp.broadcast_to(line[k : k + 1], (8, LANES))
            out_ref[k * SLICES + j, ROWS:, :] = tile.astype(out_ref.dtype)


def combine_kernel(a_ref, out_ref):
    devices = a_ref.shape[0]
    sub8 = iota((8, LANES), 0)
    parts = []
    for t in range(devices // 8):
        acc = a_ref[8 * t, ROWS:, :].astype(jnp.float32)
        for j in range(1, 8):
            acc = jnp.where(sub8 == j, a_ref[8 * t + j, ROWS:, :].astype(jnp.float32), acc)
        parts.append(acc)
    stat = jnp.concatenate(parts, axis=0)
    lse = stat + pltpu.roll(stat, LANES - 32, 1) + pltpu.roll(stat, LANES - 64, 1)
    top = jnp.max(lse, axis=0, keepdims=True)
    w = jnp.exp2(lse - top)
    w = w / jnp.sum(w, axis=0, keepdims=True)
    square = jnp.concatenate([w, jnp.zeros((LANES - devices, LANES), jnp.float32)], axis=0)
    wt = jnp.transpose(square)[:ROWS]
    acc = jnp.zeros((ROWS, LANES), jnp.float32)
    for b in range(devices):
        acc = acc + wt[:, b : b + 1] * a_ref[b, :ROWS, :].astype(jnp.float32)
    out_ref[...] = jnp.concatenate([acc[:TOK], acc[TOK:]], axis=1).astype(out_ref.dtype)


def body(queries, key_pool, value_pool, lengths, block_table):
    bf16 = jnp.bfloat16
    groups = lax.axis_size("grp")
    devices = lax.axis_size("blk")
    feats = queries.shape[1]
    first = (lax.axis_index("blk") * SLOTS).astype(jnp.int32).reshape(1)
    packed = pl.pallas_call(
        pack_kernel,
        out_shape=jax.ShapeDtypeStruct((groups, feats, LANES), bf16),
        in_specs=[VMEM],
        out_specs=VMEM,
        compiler_params=PARAMS,
        name="pack",
    )(queries.T)
    arrived = lax.all_to_all(packed, "grp", split_axis=0, concat_axis=0, tiled=True)
    spread = pl.pallas_call(
        spread_kernel,
        out_shape=jax.ShapeDtypeStruct((devices, ROWS, LANES), bf16),
        in_specs=[VMEM],
        out_specs=VMEM,
        compiler_params=PARAMS,
        name="spread",
    )(arrived.reshape(groups * feats, LANES))
    pool = (SLOTS * BLOCK, KVH * DH)
    k_hbm = in_hbm(key_pool.reshape(pool))
    v_hbm = in_hbm(value_pool.reshape(pool))
    lines = SEQS * SLICES * PART
    keys, values, gather, scatter, own, owner = pl.pallas_call(
        fetch_kernel,
        out_shape=(
            pltpu.VMEM(pool, bf16),
            pltpu.VMEM((pool[0], EARLY * DH), bf16),
            pltpu.VMEM((SLOTS * GAP, LANES), bf16),
            pltpu.VMEM((lines, LANES), bf16),
            pltpu.VMEM((SLOTS * SEQS, LANES), jnp.float32),
            pltpu.VMEM((8, LANES), jnp.int32),
        ),
        in_specs=[SMEM, HBM, HBM, HBM, HBM],
        out_specs=(VMEM,) * 6,
        scratch_shapes=[
            pltpu.SMEM(lengths.shape, jnp.int32),
            pltpu.VMEM(block_table.shape[1:], jnp.int32),
            pltpu.SemaphoreType.DMA((2, FETCHES)),
            pltpu.SemaphoreType.DMA((2,)),
        ],
        compiler_params=PARAMS,
        cost_estimate=pl.CostEstimate(flops=10**9, bytes_accessed=8 * 2**20, transcendentals=0),
        name="fetch",
    )(first, in_hbm(lengths), in_hbm(block_table[0]), k_hbm, v_hbm)
    query_all = lax.all_to_all(spread, "blk", split_axis=0, concat_axis=0, tiled=True)
    partial = pl.pallas_call(
        attend_kernel,
        out_shape=jax.ShapeDtypeStruct((devices, ROWS + 8, LANES), bf16),
        in_specs=[VMEM] * 7 + [HBM],
        out_specs=VMEM,
        scratch_shapes=[
            pltpu.VMEM((SLOTS * BLOCK, (KVH - EARLY) * DH), bf16),
            pltpu.VMEM((KVH * SLOTS, SLICES * PART, LANES), jnp.float32),
            pltpu.SemaphoreType.DMA((KVH - EARLY,)),
        ],
        compiler_params=PARAMS,
        name="attend",
    )(gather, scatter, own, owner, query_all, keys, values, v_hbm)
    collected = lax.all_to_all(partial, "blk", split_axis=0, concat_axis=0, tiled=True)
    return pl.pallas_call(
        combine_kernel,
        out_shape=jax.ShapeDtypeStruct((TOK, HEADS * DH), bf16),
        in_specs=[VMEM],
        out_specs=VMEM,
        compiler_params=PARAMS,
        name="combine",
    )(collected)


def solution(mesh):
    placed = (
        P(None, ("blk", "grp")),
        P("grp", "blk", None, None),
        P("grp", "blk", None, None),
        P("grp", None),
        P("grp", None, None),
    )
    return jax.shard_map(
        body, mesh=mesh, in_specs=placed, out_specs=P("grp", "blk"), check_vma=False
    )
```

time: 62.9 us -> 63.8 us (1.014)
  local copies, waits for them, and re-layouts: 0 us -> 0.7 us
    pallas_call x1, Pallas kernels: 3.82 us -> 4.92 us  [body(): pl.pallas_call(attend_kernel, out_shape=jax.ShapeDtypeStruct((devices, RO...]
    pallas_call x1, Pallas kernels: 0.94 us -> 0.1 us  [body(): pl.pallas_call(pack_kernel, out_shape=jax.ShapeDtypeStruct((groups, feats...]
    unnamed x0 -> x2, local copies, waits for them, and re-layouts: none -> 0.7 us
where the time goes in v4:
time: 63.8 us; the launch traced here: 63.5 us
  blocking collectives  34.2 us (54%)
  starting transfers between devices  10.2 us (16%)
  waiting for transfers between devices  9.53 us (15%)
  Pallas kernels  8.89 us (14%)
  local copies, waits for them, and re-layouts  0.7 us (1%)
    all_to_all x1, blocking collectives, body(): lax.all_to_all(packed, 'grp', split_axis=0, concat_axis=0, tiled=True)  18 us
    all_to_all x1, blocking collectives, body(): lax.all_to_all(partial, 'blk', split_axis=0, concat_axis=0, tiled=True)  16.2 us
    all_to_all x1, starting transfers between devices, body(): lax.all_to_all(spread, 'blk', split_axis=0, concat_axis=0, tiled=True)  10.2 us
    all_to_all x1, waiting for transfers between devices, body(): lax.all_to_all(spread, 'blk', split_axis=0, concat_axis=0, tiled=True)  9.53 us
    pallas_call x1, Pallas kernels, body(): pl.pallas_call(attend_kernel, out_shape=jax.ShapeDtypeStruct((devices, RO...  4.92 us
    pallas_call x1, Pallas kernels, body(): pl.pallas_call(fetch_kernel, out_shape=(pltpu.VMEM(pool, bf16), pltpu.VME...  2 us
  transfers between devices with their start and end apart: 1, of which 1 were waited for; matrix products, arithmetic and copies ran while one was open for 0% of the time, Pallas kernels for 3%

profile of v4, /device:TPU:8, one launch (start us, length us, event | category | flops | bytes accessed | tf_op | source)
XLA Modules:
  0.0 63.5 jit_solution(7776037193474067210)
XLA Ops:
  0.0 0.0 copy-start
  0.0 0.7 %copy-done = bf16[192,16]{0,1:T(8,128)(2,1)S(1)} copy-done((bf16[192,16]{0,1:T(8,128)(2,1)S(1)}, bf16[192,16]{0,1:T(8,128)(2,1)}, u32[]{:S(2)}) %copy-start) | copy-done | bytes 6168
  0.7 0.1 pack.1
  0.8 18.0 %all_to_all.15 = bf16[16,16,128]{2,1,0:T(8,128)(2,1)S(1)} all-to-all(bf16[16,16,128]{2,1,0:T(8,128)(2,1)S(1)} %pack.1), channel_id=1, replica_groups=mesh['blk'=32,'grp'=16] {'grp'}, dimensions={0} | all-to-all | bytes 131072 | tf_op jit(solution)/shard_map/all_to_all | solution.py:268
  18.8 0.8 %spread.1 = bf16[32,24,128]{2,1,0:T(8,128)(2,1)} custom-call(bf16[256,128]{1,0:T(8,128)(2,1)S(1)} %bitcast.6), custom_call_target="tpu_custom_call" | custom-call | tf_op jit(solution)/shard_map/spread/pallas_call | solution.py:269
  19.6 10.2 %all-to-all-start.1 = ((bf16[32,24,128]{2,1,0:T(8,128)(2,1)}), bf16[32,24,128]{2,1,0:T(8,128)(2,1)S(1)}, u32[]{:S(2)}, u32[]{:S(2)}) async-start(bf16[32,24,128]{2,1,0:T(8,128)(2,1)} %spread.1), calls=%async_computation.1 | async-start | bytes 393216 | tf_op jit(solution)/shard_map/all_to_all | solution.py:303
  29.8 2.0 %fetch.1 = (bf16[1024,1024]{1,0:T(8,128)(2,1)S(1)}, bf16[1024,512]{1,0:T(8,128)(2,1)S(1)}, bf16[256,128]{1,0:T(8,128)(2,1)S(1)}, bf16[96,128]{1,0:T(8,128)(2,1)S...) custom-call(s32[1]{0:T(128)} %bitcast.first_ref, s32[1,4]{1,0:T(1,128)} %len_hbm.1, s32[4,128]{1,0:T(4,128)} %bitcast.11, ...), custom_call_target="tpu_custom_call" | custom-call | flops 1000000000 | bytes 8388608 | tf_op jit(solution)/shard_map/fetch/pallas_call | solution.py:281
  31.8 9.5 %all-to-all-done.1.q_ref = bf16[32,24,128]{2,1,0:T(8,128)(2,1)S(1)} async-done(((bf16[32,24,128]{2,1,0:T(8,128)(2,1)}), bf16[32,24,128]{2,1,0:T(8,128)(2,1)S(1)}, u32[]{:S(2)}, u32[]{:S(2)}) %all-to-all-start.1) | async-done | bytes 196640 | tf_op jit(solution)/shard_map/all_to_all | solution.py:303
  41.4 4.9 %attend.1 = bf16[32,32,128]{2,1,0:T(8,128)(2,1)S(1)} custom-call(bf16[256,128]{1,0:T(8,128)(2,1)S(1)} %get-tuple-element.11.gather_ref, bf16[96,128]{1,0:T(8,128)(2,1)S(1)} %get-tuple-element.12.scatter_ref, f32[32,128]{1,0:T(8,128)S(1)} %get-tuple-element.13.own_ref, s32[8,128]{1,0:T(8,128)S(1)} %get-tuple-element.14.owner_ref, ...), custom_call_target="tpu_custom_call" | custom-call | tf_op jit(solution)/shard_map/attend/pallas_call | solution.py:304
  46.3 16.2 %all_to_all.16.a_ref = bf16[32,32,128]{2,1,0:T(8,128)(2,1)S(1)} all-to-all(bf16[32,32,128]{2,1,0:T(8,128)(2,1)S(1)} %attend.1), channel_id=1, replica_groups=mesh['blk'=32,'grp'=16] {'blk'}, dimensions={0} | all-to-all | bytes 524288 | tf_op jit(solution)/shard_map/all_to_all | solution.py:317
  62.5 1.0 %combine.1 = bf16[12,256]{1,0:T(8,128)(2,1)} custom-call(bf16[32,32,128]{2,1,0:T(8,128)(2,1)S(1)} %all_to_all.16.a_ref), custom_call_target="tpu_custom_call" | custom-call | tf_op jit(solution)/shard_map/combine/pallas_call | solution.py:318
Async XLA Ops:
  0.0 0.7 %copy-start = (bf16[192,16]{0,1:T(8,128)(2,1)S(1)}, bf16[192,16]{0,1:T(8,128)(2,1)}, u32[]{:S(2)}) copy-start(bf16[192,16]{0,1:T(8,128)(2,1)} %param.5) | copy-start | bytes 18436
  19.6 21.7 %all-to-all-start.1 = ((bf16[32,24,128]{2,1,0:T(8,128)(2,1)}), bf16[32,24,128]{2,1,0:T(8,128)(2,1)S(1)}, u32[]{:S(2)}, u32[]{:S(2)}) async-start(bf16[32,24,128]{2,1,0:T(8,128)(2,1)} %spread.1), calls=%async_computation.1 | async-start | bytes 393216 | tf_op jit(solution)/shard_map/all_to_all | solution.py:303

commit v5 on v1

--- a/solution.py
+++ b/solution.py
@@ -17,14 +17,27 @@
 ROWS = HEADS * TOK
 SLICES = 4
 SLOTS = 8
+WIDE = 256
+CHUNK = 16
 BLOCK = 128
+FETCHES = 8
+LATE = 6
+EARLY = 4
 LANES = 128
 SCALE = math.log2(math.e) / math.sqrt(DH)
 LN2 = math.log(2.0)
 EMPTY = -1e30
 
 VMEM = pl.BlockSpec(memory_space=pltpu.VMEM)
+HBM = pl.BlockSpec(memory_space=pltpu.HBM)
 SMEM = pl.BlockSpec(memory_space=pltpu.SMEM)
+
+
+PARAMS = pltpu.CompilerParams(vmem_limit_bytes=16 * 1024 * 1024)
+
+
+def in_hbm(array):
+    return pltpu.with_memory_space_constraint(array, pltpu.HBM)
 
 
 def iota(shape, dim):
@@ -54,7 +67,26 @@
         out_ref[b] = rows
 
 
-def attend_kernel(first_ref, len_ref, table_ref, q_ref, k_ref, v_ref, out_ref):
+def fetch_kernel(
+    first_ref, len_hbm, table_hbm, k_hbm, v_hbm,
+    k_ref, v_ref, bias_ref, len_ref, table_ref, sems, small,
+):
+    rows = k_ref.shape[0] // FETCHES
+    copies = []
+    for i in range(FETCHES):
+        at = pl.ds(i * rows, rows)
+        copies.append(pltpu.make_async_copy(k_hbm.at[at], k_ref.at[at], sems.at[0, i]))
+        copies.append(
+            pltpu.make_async_copy(v_hbm.at[at, pl.ds(0, EARLY * DH)], v_ref.at[at], sems.at[1, i])
+        )
+    facts = [
+        pltpu.make_async_copy(table_hbm, table_ref, small.at[0]),
+        pltpu.make_async_copy(len_hbm, len_ref, small.at[1]),
+    ]
+    for c in facts + copies:
+        c.start()
+    for c in facts:
+        c.wait()
     lane4 = iota((SEQS, LANES), 1)
     sub4 = iota((SEQS, LANES), 0)
     lens = jnp.zeros((SEQS, LANES), jnp.int32)
@@ -63,33 +95,85 @@
     local = jnp.where(lane4 < lens, table_ref[...] - first_ref[0], -1)
     row = iota((ROWS, LANES), 0)
     seq = jnp.where(row >= TOK, row - TOK, row) // STEPS
-    bias = []
     for s in range(SLOTS):
         hit = jnp.max((local == s).astype(jnp.float32), axis=1, keepdims=True)
         off = jnp.broadcast_to(jnp.where(hit > 0.0, 0.0, EMPTY), (SEQS, LANES))
         b = jnp.broadcast_to(off[0:1], (ROWS, LANES))
         for q in range(1, SEQS):
             b = jnp.where(seq == q, off[q : q + 1], b)
-        bias.append(b)
-    bias = jnp.concatenate(bias, axis=1)
-    bias = jnp.concatenate([bias] * SLICES, axis=0)
-
+        bias_ref[:, s * BLOCK : (s + 1) * BLOCK] = b
+    for c in copies:
+        c.wait()
+
+
+def attend_kernel(
+    bias_ref, q_ref, k_ref, v_ref, v_hbm, out_ref, late_ref, s_ref, p_ref, top_ref, sum_ref, sems
+):
+    late = []
+    for k in range(EARLY, KVH):
+        to = pl.ds((k - EARLY) * DH, DH)
+        late.append(
+            pltpu.make_async_copy(
+                v_hbm.at[:, pl.ds(k * DH, DH)], late_ref.at[:, to], sems.at[k - EARLY]
+            )
+        )
+        late[-1].start()
     rows = SLICES * ROWS
     lane = iota((rows, LANES), 1)
     lse = jnp.zeros((rows, LANES), jnp.float32)
     nt = (((1,), (1,)), ((), ()))
     nn = (((1,), (0,)), ((), ()))
-    for k in range(KVH):
-        cols = slice(k * DH, (k + 1) * DH)
+
+    def cols(k):
+        return slice(k * DH, (k + 1) * DH)
+
+    def scores(k):
         qk = q_ref[k * SLICES : (k + 1) * SLICES].reshape(rows, DH)
-        s = lax.dot_general(qk, k_ref[:, cols], nt, preferred_element_type=jnp.float32) + bias
-        top = jnp.max(s, axis=1, keepdims=True)
-        p = jnp.exp2((s - top) * SCALE).astype(jnp.bfloat16)
-        total = jnp.sum(p.astype(jnp.float32), axis=1, keepdims=True)
-        o = lax.dot_general(p, v_ref[:, cols], nn, preferred_element_type=jnp.float32)
-        o = (o / total).astype(out_ref.dtype)
-        lse = jnp.where(lane == k, top * SCALE + jnp.log2(total), lse)
+        most = None
+        for j in range(0, SLOTS * BLOCK, WIDE):
+            at = slice(j, j + WIDE)
+            s = lax.dot_general(qk, k_ref[at, cols(k)], nt, preferred_element_type=jnp.float32)
+            s = s + jnp.concatenate([bias_ref[:, at]] * SLICES, axis=0)
+            s_ref[k % 2, :, at] = s
+            for i in range(0, WIDE, LANES):
+                part = s[:, i : i + LANES]
+                most = part if most is None else jnp.maximum(most, part)
+        top = jnp.max(most, axis=1, keepdims=True)
+        top_ref[k] = jnp.broadcast_to(top, (rows, LANES))
+
+    def weights(k):
+        for r in range(0, rows, CHUNK):
+            at = slice(r, r + CHUNK)
+            top = top_ref[k, at]
+            total = None
+            for j in range(0, SLOTS * BLOCK, LANES):
+                here = slice(j, j + LANES)
+                p = jnp.exp2((s_ref[k % 2, at, here] - top) * SCALE)
+                total = p if total is None else total + p
+                p_ref[k % 2, at, here] = p.astype(jnp.bfloat16)
+            sum_ref[k % 2, at] = total
+
+    def values(k, lse):
+        if k < EARLY:
+            v = v_ref[:, cols(k)]
+        else:
+            v = late_ref[:, cols(k - EARLY)]
+        o = lax.dot_general(p_ref[k % 2], v, nn, preferred_element_type=jnp.float32)
+        total = jnp.sum(sum_ref[k % 2], axis=1, keepdims=True)
+        o = (o * (1.0 / total)).astype(out_ref.dtype)
         out_ref[k * SLICES : (k + 1) * SLICES, :ROWS, :] = o.reshape(SLICES, ROWS, DH)
+        return jnp.where(lane == k, top_ref[k] * SCALE + jnp.log2(total), lse)
+
+    for step in range(KVH + 2):
+        if step == LATE:
+            for c in late:
+                c.wait()
+        if step < KVH:
+            scores(step)
+        if 0 <= step - 1 < KVH:
+            weights(step - 1)
+        if step >= 2:
+            lse = values(step - 2, lse)
     square = jnp.concatenate([lse, jnp.zeros((LANES - rows, LANES), jnp.float32)], axis=0)
     flat = jnp.transpose(square)[:KVH]
     lane8 = iota((KVH, LANES), 1)
@@ -133,11 +217,13 @@
     groups = lax.axis_size("grp")
     devices = lax.axis_size("blk")
     feats = queries.shape[1]
+    first = (lax.axis_index("blk") * SLOTS).astype(jnp.int32).reshape(1)
     packed = pl.pallas_call(
         pack_kernel,
         out_shape=jax.ShapeDtypeStruct((groups, feats, LANES), bf16),
         in_specs=[VMEM],
         out_specs=VMEM,
+        compiler_params=PARAMS,
         name="pack",
     )(queries.T)
     arrived = lax.all_to_all(packed, "grp", split_axis=0, concat_axis=0, tiled=True)
@@ -146,30 +232,56 @@
         out_shape=jax.ShapeDtypeStruct((devices, ROWS, LANES), bf16),
         in_specs=[VMEM],
         out_specs=VMEM,
+        compiler_params=PARAMS,
         name="spread",
     )(arrived.reshape(groups * feats, LANES))
+    pool = (SLOTS * BLOCK, KVH * DH)
+    k_hbm = in_hbm(key_pool.reshape(pool))
+    v_hbm = in_hbm(value_pool.reshape(pool))
+    keys, values, bias = pl.pallas_call(
+        fetch_kernel,
+        out_shape=(
+            pltpu.VMEM(pool, bf16),
+            pltpu.VMEM((pool[0], EARLY * DH), bf16),
+            pltpu.VMEM((ROWS, pool[0]), jnp.float32),
+        ),
+        in_specs=[SMEM, HBM, HBM, HBM, HBM],
+        out_specs=(VMEM,) * 3,
+        scratch_shapes=[
+            pltpu.SMEM(lengths.shape, jnp.int32),
+            pltpu.VMEM(block_table.shape[1:], jnp.int32),
+            pltpu.SemaphoreType.DMA((2, FETCHES)),
+            pltpu.SemaphoreType.DMA((2,)),
+        ],
+        compiler_params=PARAMS,
+        cost_estimate=pl.CostEstimate(flops=10**9, bytes_accessed=8 * 2**20, transcendentals=0),
+        name="fetch",
+    )(first, in_hbm(lengths), in_hbm(block_table[0]), k_hbm, v_hbm)
     query_all = lax.all_to_all(spread, "blk", split_axis=0, concat_axis=0, tiled=True)
-    first = (lax.axis_index("blk") * SLOTS).astype(jnp.int32).reshape(1)
+    rows = SLICES * ROWS
     partial = pl.pallas_call(
         attend_kernel,
         out_shape=jax.ShapeDtypeStruct((devices, ROWS + 8, LANES), bf16),
-        in_specs=[SMEM, SMEM, VMEM, VMEM, VMEM, VMEM],
-        out_specs=VMEM,
+        in_specs=[VMEM] * 4 + [HBM],
+        out_specs=VMEM,
+        scratch_shapes=[
+            pltpu.VMEM((pool[0], (KVH - EARLY) * DH), bf16),
+            pltpu.VMEM((2, rows, pool[0]), jnp.float32),
+            pltpu.VMEM((2, rows, pool[0]), bf16),
+            pltpu.VMEM((KVH, rows, LANES), jnp.float32),
+            pltpu.VMEM((2, rows, LANES), jnp.float32),
+            pltpu.SemaphoreType.DMA((KVH - EARLY,)),
+        ],
+        compiler_params=PARAMS,
         name="attend",
-    )(
-        first,
-        lengths,
-        block_table[0],
-        query_all,
-        key_pool.reshape(SLOTS * BLOCK, KVH * DH),
-        value_pool.reshape(SLOTS * BLOCK, KVH * DH),
-    )
+    )(bias, query_all, keys, values, v_hbm)
     collected = lax.all_to_all(partial, "blk", split_axis=0, concat_axis=0, tiled=True)
     return pl.pallas_call(
         combine_kernel,
         out_shape=jax.ShapeDtypeStruct((TOK, HEADS * DH), bf16),
         in_specs=[VMEM],
         out_specs=VMEM,
+        compiler_params=PARAMS,
         name="combine",
     )(collected)
 

time: 68.8 us -> 61.2 us (0.89)
  Pallas kernels: 11.2 us -> 6.26 us
  waiting for transfers between devices: 11.5 us -> 9.53 us
    pallas_call x1, Pallas kernels: 6.14 us -> 2.29 us  [body(): pl.pallas_call(attend_kernel, out_shape=jax.ShapeDtypeStruct((devices, RO...]
    all_to_all x1, waiting for transfers between devices: 11.5 us -> 9.53 us  [body(): lax.all_to_all(spread, 'blk', split_axis=0, concat_axis=0, tiled=True)]
    pallas_call x0 -> x1, Pallas kernels: none -> 2 us  [body(): pl.pallas_call(fetch_kernel, out_shape=(pltpu.VMEM(pool, bf16), pltpu.VME...]
    pallas_call x1, Pallas kernels: 1.41 us -> 0.1 us  [body(): pl.pallas_call(pack_kernel, out_shape=jax.ShapeDtypeStruct((groups, feats...]
    pallas_call x1, Pallas kernels: 1.98 us -> 1.04 us  [body(): pl.pallas_call(combine_kernel, out_shape=jax.ShapeDtypeStruct((TOK, HEADS...]
    pallas_call x1, Pallas kernels: 1.67 us -> 0.83 us  [body(): pl.pallas_call(spread_kernel, out_shape=jax.ShapeDtypeStruct((devices, RO...]
  transfers between devices with their start and end apart: 1 -> 1, of which waited for: 1 -> 1; matrix products, arithmetic and copies ran while one was open for 0% -> 0% of each run, Pallas kernels for 0% -> 3%
where the time goes in v5:
time: 61.2 us; the launch traced here: 60.9 us
  blocking collectives  34.2 us (56%)
  starting transfers between devices  10.2 us (17%)
  waiting for transfers between devices  9.53 us (16%)
  Pallas kernels  6.26 us (10%)
  local copies, waits for them, and re-layouts  0.7 us (1%)
    all_to_all x1, blocking collectives, body(): lax.all_to_all(packed, 'grp', split_axis=0, concat_axis=0, tiled=True)  18 us
    all_to_all x1, blocking collectives, body(): lax.all_to_all(partial, 'blk', split_axis=0, concat_axis=0, tiled=True)  16.1 us
    all_to_all x1, starting transfers between devices, body(): lax.all_to_all(spread, 'blk', split_axis=0, concat_axis=0, tiled=True)  10.2 us
    all_to_all x1, waiting for transfers between devices, body(): lax.all_to_all(spread, 'blk', split_axis=0, concat_axis=0, tiled=True)  9.53 us
    pallas_call x1, Pallas kernels, body(): pl.pallas_call(attend_kernel, out_shape=jax.ShapeDtypeStruct((devices, RO...  2.29 us
    pallas_call x1, Pallas kernels, body(): pl.pallas_call(fetch_kernel, out_shape=(pltpu.VMEM(pool, bf16), pltpu.VME...  2 us
  transfers between devices with their start and end apart: 1, of which 1 were waited for; matrix products, arithmetic and copies ran while one was open for 0% of the time, Pallas kernels for 3%

profile of v5, /device:TPU:8, one launch (start us, length us, event | category | flops | bytes accessed | tf_op | source)
XLA Modules:
  0.0 60.9 jit_solution(5089630596464147882)
XLA Ops:
  0.0 0.0 copy-start
  0.0 0.7 %copy-done = bf16[192,16]{0,1:T(8,128)(2,1)S(1)} copy-done((bf16[192,16]{0,1:T(8,128)(2,1)S(1)}, bf16[192,16]{0,1:T(8,128)(2,1)}, u32[]{:S(2)}) %copy-start) | copy-done | bytes 6168
  0.7 0.1 pack.1
  0.8 18.0 %all_to_all.15 = bf16[16,16,128]{2,1,0:T(8,128)(2,1)S(1)} all-to-all(bf16[16,16,128]{2,1,0:T(8,128)(2,1)S(1)} %pack.1), channel_id=1, replica_groups=mesh['blk'=32,'grp'=16] {'grp'}, dimensions={0} | all-to-all | bytes 131072 | tf_op jit(solution)/shard_map/all_to_all | solution.py:229
  18.8 0.8 %spread.1 = bf16[32,24,128]{2,1,0:T(8,128)(2,1)} custom-call(bf16[256,128]{1,0:T(8,128)(2,1)S(1)} %bitcast.6), custom_call_target="tpu_custom_call" | custom-call | tf_op jit(solution)/shard_map/spread/pallas_call | solution.py:230
  19.6 10.2 %all-to-all-start.1 = ((bf16[32,24,128]{2,1,0:T(8,128)(2,1)}), bf16[32,24,128]{2,1,0:T(8,128)(2,1)S(1)}, u32[]{:S(2)}, u32[]{:S(2)}) async-start(bf16[32,24,128]{2,1,0:T(8,128)(2,1)} %spread.1), calls=%async_computation.1 | async-start | bytes 393216 | tf_op jit(solution)/shard_map/all_to_all | solution.py:260
  29.8 2.0 %fetch.1 = (bf16[1024,1024]{1,0:T(8,128)(2,1)S(1)}, bf16[1024,512]{1,0:T(8,128)(2,1)S(1)}, f32[24,1024]{1,0:T(8,128)S(1)}) custom-call(s32[1]{0:T(128)} %bitcast.first_ref, s32[1,4]{1,0:T(1,128)} %len_hbm.1, s32[4,128]{1,0:T(4,128)} %bitcast.11, bf16[1024,1024]{1,0:T(8,128)(2,1)} %bitcast.10, bf16[1024,1024]{1,0:T(8,128)(2,1)} %bitcast.8), custom_call_target="tpu_custom_call" | custom-call | flops 1000000000 | bytes 8388608 | tf_op jit(solution)/shard_map/fetch/pallas_call | solution.py:241
  31.8 9.5 %all-to-all-done.1.q_ref = bf16[32,24,128]{2,1,0:T(8,128)(2,1)S(1)} async-done(((bf16[32,24,128]{2,1,0:T(8,128)(2,1)}), bf16[32,24,128]{2,1,0:T(8,128)(2,1)S(1)}, u32[]{:S(2)}, u32[]{:S(2)}) %all-to-all-start.1) | async-done | bytes 196640 | tf_op jit(solution)/shard_map/all_to_all | solution.py:260
  41.4 2.3 %attend.1 = bf16[32,32,128]{2,1,0:T(8,128)(2,1)S(1)} custom-call(f32[24,1024]{1,0:T(8,128)S(1)} %get-tuple-element.8.bias_ref, bf16[32,24,128]{2,1,0:T(8,128)(2,1)S(1)} %all-to-all-done.1.q_ref, bf16[1024,1024]{1,0:T(8,128)(2,1)S(1)} %get-tuple-element.9.k_ref, bf16[1024,512]{1,0:T(8,128)(2,1)S(1)} %get-tuple-element.10.v_ref, bf16[1024,1024]{1,0:T(8,128)(2,1)} %bitcast.9), custom_call_target="tpu_custom_call" | custom-call | tf_op jit(solution)/shard_map/attend/pallas_call | solution.py:262
  43.7 16.1 %all_to_all.16.a_ref = bf16[32,32,128]{2,1,0:T(8,128)(2,1)S(1)} all-to-all(bf16[32,32,128]{2,1,0:T(8,128)(2,1)S(1)} %attend.1), channel_id=1, replica_groups=mesh['blk'=32,'grp'=16] {'blk'}, dimensions={0} | all-to-all | bytes 524288 | tf_op jit(solution)/shard_map/all_to_all | solution.py:278
  59.8 1.0 %combine.1 = bf16[12,256]{1,0:T(8,128)(2,1)} custom-call(bf16[32,32,128]{2,1,0:T(8,128)(2,1)S(1)} %all_to_all.16.a_ref), custom_call_target="tpu_custom_call" | custom-call | tf_op jit(solution)/shard_map/combine/pallas_call | solution.py:279
Async XLA Ops:
  0.0 0.7 %copy-start = (bf16[192,16]{0,1:T(8,128)(2,1)S(1)}, bf16[192,16]{0,1:T(8,128)(2,1)}, u32[]{:S(2)}) copy-start(bf16[192,16]{0,1:T(8,128)(2,1)} %param.5) | copy-start | bytes 18436
  19.6 21.7 %all-to-all-start.1 = ((bf16[32,24,128]{2,1,0:T(8,128)(2,1)}), bf16[32,24,128]{2,1,0:T(8,128)(2,1)S(1)}, u32[]{:S(2)}, u32[]{:S(2)}) async-start(bf16[32,24,128]{2,1,0:T(8,128)(2,1)} %spread.1), calls=%async_computation.1 | async-start | bytes 393216 | tf_op jit(solution)/shard_map/all_to_all | solution.py:260

commit v6 on v5

--- a/solution.py
+++ b/solution.py
@@ -24,6 +24,8 @@
 LATE = 6
 EARLY = 4
 LANES = 128
+HALF_FEATS = 8
+HALF = 16
 SCALE = math.log2(math.e) / math.sqrt(DH)
 LN2 = math.log(2.0)
 EMPTY = -1e30
@@ -47,22 +49,41 @@
 def pack_kernel(q_ref, out_ref):
     groups, feats, _ = out_ref.shape
     q = q_ref[...].astype(jnp.float32)
-    keep = iota((feats, LANES), 1) < TOK
-    wide = jnp.concatenate([q, jnp.zeros((feats, 2 * LANES - q.shape[1]), jnp.float32)], axis=1)
+    lane = iota((feats, LANES), 1)
+    wide = jnp.concatenate([q, jnp.zeros((2 * feats, 2 * LANES - q.shape[1]), jnp.float32)], axis=1)
+
+    def turned(part, shift):
+        shift %= 2 * LANES
+        return (part if shift == 0 else pltpu.roll(part, shift, 1))[:, :LANES]
+
     for g in range(groups):
-        at = g * TOK
-        shifted = wide if at == 0 else pltpu.roll(wide, 2 * LANES - at, 1)
-        out_ref[g] = jnp.where(keep, shifted[:, :LANES], 0.0).astype(out_ref.dtype)
+        low = turned(wide[:feats], -g * TOK)
+        high = turned(wide[feats:], HALF - g * TOK)
+        both = jnp.where(lane < TOK, low, jnp.where((lane >= HALF) & (lane < HALF + TOK), high, 0.0))
+        out_ref[g] = both.astype(out_ref.dtype)
 
 
 def spread_kernel(a_ref, out_ref):
+    feats = a_ref.shape[0]
     row = iota((ROWS, LANES), 0)
     tok = jnp.where(row >= TOK, row - TOK, row)
-    pick = (tok == iota((ROWS, LANES), 1)).astype(jnp.bfloat16)
+    lane = iota((ROWS, LANES), 1)
     nt = (((1,), (1,)), ((), ()))
-    first = lax.dot_general(pick, a_ref[:LANES, :], nt, preferred_element_type=jnp.float32)
-    second = lax.dot_general(pick, a_ref[LANES:, :], nt, preferred_element_type=jnp.float32)
-    rows = jnp.where(row < TOK, first, second).astype(out_ref.dtype)
+    nn = (((1,), (0,)), ((), ()))
+    halves = []
+    for j in range(2):
+        pick = (lane == tok + j * HALF).astype(jnp.bfloat16)
+        halves.append(lax.dot_general(pick, a_ref[...], nt, preferred_element_type=jnp.float32))
+    apart = jnp.concatenate(halves, axis=1).astype(jnp.bfloat16)
+    at = iota((2 * feats, 2 * feats), 0)
+    to = iota((2 * feats, 2 * feats), 1)
+    second = at >= feats
+    at = jnp.where(second, at - feats, at)
+    order = to == (at // HALF_FEATS) * (2 * HALF_FEATS) + at % HALF_FEATS + jnp.where(second, HALF_FEATS, 0)
+    whole = lax.dot_general(
+        apart, order.astype(jnp.bfloat16), nn, preferred_element_type=jnp.float32
+    )
+    rows = jnp.where(row < TOK, whole[:, :LANES], whole[:, LANES:]).astype(out_ref.dtype)
     for b in range(out_ref.shape[0]):
         out_ref[b] = rows
 
@@ -141,7 +162,7 @@
         top = jnp.max(most, axis=1, keepdims=True)
         top_ref[k] = jnp.broadcast_to(top, (rows, LANES))
 
-    def weights(k):
+    def weights(k, lse):
         for r in range(0, rows, CHUNK):
             at = slice(r, r + CHUNK)
             top = top_ref[k, at]
@@ -151,18 +172,19 @@
                 p = jnp.exp2((s_ref[k % 2, at, here] - top) * SCALE)
                 total = p if total is None else total + p
                 p_ref[k % 2, at, here] = p.astype(jnp.bfloat16)
-            sum_ref[k % 2, at] = total
-
-    def values(k, lse):
+            sum_ref[k % 2, at] = jnp.broadcast_to(
+                jnp.sum(total, axis=1, keepdims=True), (CHUNK, LANES)
+            )
+        return jnp.where(lane == k, top_ref[k] * SCALE + jnp.log2(sum_ref[k % 2]), lse)
+
+    def values(k):
         if k < EARLY:
             v = v_ref[:, cols(k)]
         else:
             v = late_ref[:, cols(k - EARLY)]
         o = lax.dot_general(p_ref[k % 2], v, nn, preferred_element_type=jnp.float32)
-        total = jnp.sum(sum_ref[k % 2], axis=1, keepdims=True)
-        o = (o * (1.0 / total)).astype(out_ref.dtype)
+        o = (o * (1.0 / sum_ref[k % 2])).astype(out_ref.dtype)
         out_ref[k * SLICES : (k + 1) * SLICES, :ROWS, :] = o.reshape(SLICES, ROWS, DH)
-        return jnp.where(lane == k, top_ref[k] * SCALE + jnp.log2(total), lse)
 
     for step in range(KVH + 2):
         if step == LATE:
@@ -171,9 +193,9 @@
         if step < KVH:
             scores(step)
         if 0 <= step - 1 < KVH:
-            weights(step - 1)
+            lse = weights(step - 1, lse)
         if step >= 2:
-            lse = values(step - 2, lse)
+            values(step - 2)
     square = jnp.concatenate([lse, jnp.zeros((LANES - rows, LANES), jnp.float32)], axis=0)
     flat = jnp.transpose(square)[:KVH]
     lane8 = iota((KVH, LANES), 1)
@@ -216,11 +238,10 @@
     bf16 = jnp.bfloat16
     groups = lax.axis_size("grp")
     devices = lax.axis_size("blk")
-    feats = queries.shape[1]
     first = (lax.axis_index("blk") * SLOTS).astype(jnp.int32).reshape(1)
     packed = pl.pallas_call(
         pack_kernel,
-        out_shape=jax.ShapeDtypeStruct((groups, feats, LANES), bf16),
+        out_shape=jax.ShapeDtypeStruct((groups, HALF_FEATS, LANES), bf16),
         in_specs=[VMEM],
         out_specs=VMEM,
         compiler_params=PARAMS,
@@ -234,7 +255,7 @@
         out_specs=VMEM,
         compiler_params=PARAMS,
         name="spread",
-    )(arrived.reshape(groups * feats, LANES))
+    )(arrived.reshape(groups * HALF_FEATS, LANES))
     pool = (SLOTS * BLOCK, KVH * DH)
     k_hbm = in_hbm(key_pool.reshape(pool))
     v_hbm = in_hbm(value_pool.reshape(pool))

time: 61.2 us -> 61.6 us (level)
  Pallas kernels: 6.26 us -> 7.29 us
    pallas_call x1, Pallas kernels: 2.29 us -> 3.17 us  [body(): pl.pallas_call(attend_kernel, out_shape=jax.ShapeDtypeStruct((devices, RO...]
where the time goes in v6:
time: 61.6 us; the launch traced here: 61.3 us
  blocking collectives  33.9 us (55%)
  starting transfers between devices  10.2 us (17%)
  waiting for transfers between devices  9.25 us (15%)
  Pallas kernels  7.29 us (12%)
  local copies, waits for them, and re-layouts  0.7 us (1%)
    all_to_all x1, blocking collectives, body(): lax.all_to_all(packed, 'grp', split_axis=0, concat_axis=0, tiled=True)  17.9 us
    all_to_all x1, blocking collectives, body(): lax.all_to_all(partial, 'blk', split_axis=0, concat_axis=0, tiled=True)  16 us
    all_to_all x1, starting transfers between devices, body(): lax.all_to_all(spread, 'blk', split_axis=0, concat_axis=0, tiled=True)  10.2 us
    all_to_all x1, waiting for transfers between devices, body(): lax.all_to_all(spread, 'blk', split_axis=0, concat_axis=0, tiled=True)  9.25 us
    pallas_call x1, Pallas kernels, body(): pl.pallas_call(attend_kernel, out_shape=jax.ShapeDtypeStruct((devices, RO...  3.17 us
    pallas_call x1, Pallas kernels, body(): pl.pallas_call(fetch_kernel, out_shape=(pltpu.VMEM(pool, bf16), pltpu.VME...  2 us
  transfers between devices with their start and end apart: 1, of which 1 were waited for; matrix products, arithmetic and copies ran while one was open for 0% of the time, Pallas kernels for 3%

profile of v6, /device:TPU:8, one launch (start us, length us, event | category | flops | bytes accessed | tf_op | source)
XLA Modules:
  0.0 61.3 jit_solution(3172683512528506749)
XLA Ops:
  0.0 0.0 copy-start
  0.0 0.7 %copy-done = bf16[192,16]{0,1:T(8,128)(2,1)S(1)} copy-done((bf16[192,16]{0,1:T(8,128)(2,1)S(1)}, bf16[192,16]{0,1:T(8,128)(2,1)}, u32[]{:S(2)}) %copy-start) | copy-done | bytes 6168
  0.7 0.1 pack.1
  0.8 17.9 %all_to_all.15 = bf16[16,8,128]{2,1,0:T(8,128)(2,1)S(1)} all-to-all(bf16[16,8,128]{2,1,0:T(8,128)(2,1)S(1)} %pack.1), channel_id=1, replica_groups=mesh['blk'=32,'grp'=16] {'grp'}, dimensions={0} | all-to-all | bytes 65536 | tf_op jit(solution)/shard_map/all_to_all | solution.py:250
  18.7 1.0 %spread.1 = bf16[32,24,128]{2,1,0:T(8,128)(2,1)} custom-call(bf16[128,128]{1,0:T(8,128)(2,1)S(1)} %bitcast.6), custom_call_target="tpu_custom_call" | custom-call | tf_op jit(solution)/shard_map/spread/pallas_call | solution.py:251
  19.7 10.2 %all-to-all-start.1 = ((bf16[32,24,128]{2,1,0:T(8,128)(2,1)}), bf16[32,24,128]{2,1,0:T(8,128)(2,1)S(1)}, u32[]{:S(2)}, u32[]{:S(2)}) async-start(bf16[32,24,128]{2,1,0:T(8,128)(2,1)} %spread.1), calls=%async_computation.1 | async-start | bytes 393216 | tf_op jit(solution)/shard_map/all_to_all | solution.py:281
  29.9 2.0 %fetch.1 = (bf16[1024,1024]{1,0:T(8,128)(2,1)S(1)}, bf16[1024,512]{1,0:T(8,128)(2,1)S(1)}, f32[24,1024]{1,0:T(8,128)S(1)}) custom-call(s32[1]{0:T(128)} %bitcast.first_ref, s32[1,4]{1,0:T(1,128)} %len_hbm.1, s32[4,128]{1,0:T(4,128)} %bitcast.11, bf16[1024,1024]{1,0:T(8,128)(2,1)} %bitcast.10, bf16[1024,1024]{1,0:T(8,128)(2,1)} %bitcast.8), custom_call_target="tpu_custom_call" | custom-call | flops 1000000000 | bytes 8388608 | tf_op jit(solution)/shard_map/fetch/pallas_call | solution.py:262
  31.9 9.2 %all-to-all-done.1.q_ref = bf16[32,24,128]{2,1,0:T(8,128)(2,1)S(1)} async-done(((bf16[32,24,128]{2,1,0:T(8,128)(2,1)}), bf16[32,24,128]{2,1,0:T(8,128)(2,1)S(1)}, u32[]{:S(2)}, u32[]{:S(2)}) %all-to-all-start.1) | async-done | bytes 196640 | tf_op jit(solution)/shard_map/all_to_all | solution.py:281
  41.1 3.2 %attend.1 = bf16[32,32,128]{2,1,0:T(8,128)(2,1)S(1)} custom-call(f32[24,1024]{1,0:T(8,128)S(1)} %get-tuple-element.8.bias_ref, bf16[32,24,128]{2,1,0:T(8,128)(2,1)S(1)} %all-to-all-done.1.q_ref, bf16[1024,1024]{1,0:T(8,128)(2,1)S(1)} %get-tuple-element.9.k_ref, bf16[1024,512]{1,0:T(8,128)(2,1)S(1)} %get-tuple-element.10.v_ref, bf16[1024,1024]{1,0:T(8,128)(2,1)} %bitcast.9), custom_call_target="tpu_custom_call" | custom-call | tf_op jit(solution)/shard_map/attend/pallas_call | solution.py:283
  44.3 16.0 %all_to_all.16.a_ref = bf16[32,32,128]{2,1,0:T(8,128)(2,1)S(1)} all-to-all(bf16[32,32,128]{2,1,0:T(8,128)(2,1)S(1)} %attend.1), channel_id=1, replica_groups=mesh['blk'=32,'grp'=16] {'blk'}, dimensions={0} | all-to-all | bytes 524288 | tf_op jit(solution)/shard_map/all_to_all | solution.py:299
  60.3 1.0 %combine.1 = bf16[12,256]{1,0:T(8,128)(2,1)} custom-call(bf16[32,32,128]{2,1,0:T(8,128)(2,1)S(1)} %all_to_all.16.a_ref), custom_call_target="tpu_custom_call" | custom-call | tf_op jit(solution)/shard_map/combine/pallas_call | solution.py:300
Async XLA Ops:
  0.0 0.7 %copy-start = (bf16[192,16]{0,1:T(8,128)(2,1)S(1)}, bf16[192,16]{0,1:T(8,128)(2,1)}, u32[]{:S(2)}) copy-start(bf16[192,16]{0,1:T(8,128)(2,1)} %param.5) | copy-start | bytes 18436
  19.7 21.4 %all-to-all-start.1 = ((bf16[32,24,128]{2,1,0:T(8,128)(2,1)}), bf16[32,24,128]{2,1,0:T(8,128)(2,1)S(1)}, u32[]{:S(2)}, u32[]{:S(2)}) async-start(bf16[32,24,128]{2,1,0:T(8,128)(2,1)} %spread.1), calls=%async_computation.1 | async-start | bytes 393216 | tf_op jit(solution)/shard_map/all_to_all | solution.py:281

commit v7 on v6

--- a/solution.py
+++ b/solution.py
@@ -130,15 +130,18 @@
 def attend_kernel(
     bias_ref, q_ref, k_ref, v_ref, v_hbm, out_ref, late_ref, s_ref, p_ref, top_ref, sum_ref, sems
 ):
-    late = []
-    for k in range(EARLY, KVH):
-        to = pl.ds((k - EARLY) * DH, DH)
-        late.append(
-            pltpu.make_async_copy(
-                v_hbm.at[:, pl.ds(k * DH, DH)], late_ref.at[:, to], sems.at[k - EARLY]
-            )
+    def late(k):
+        return pltpu.make_async_copy(
+            v_hbm.at[:, pl.ds(pl.multiple_of((EARLY + k) * DH, DH), DH)],
+            late_ref.at[:, pl.ds(pl.multiple_of(k * DH, DH), DH)],
+            sems.at[k],
         )
-        late[-1].start()
+
+    def send_for(k, carry):
+        late(k).start()
+        return carry
+
+    lax.fori_loop(0, KVH - EARLY, send_for, 0)
     rows = SLICES * ROWS
     lane = iota((rows, LANES), 1)
     lse = jnp.zeros((rows, LANES), jnp.float32)
@@ -188,8 +191,8 @@
 
     for step in range(KVH + 2):
         if step == LATE:
-            for c in late:
-                c.wait()
+            for k in range(KVH - EARLY):
+                late(k).wait()
         if step < KVH:
             scores(step)
         if 0 <= step - 1 < KVH:

time: 61.6 us -> 60.6 us (0.984)
  Pallas kernels: 7.29 us -> 6.32 us
    pallas_call x1, Pallas kernels: 3.17 us -> 2.2 us  [body(): pl.pallas_call(attend_kernel, out_shape=jax.ShapeDtypeStruct((devices, RO...]
where the time goes in v7:
time: 60.6 us; the launch traced here: 60.3 us
  blocking collectives  33.9 us (56%)
  starting transfers between devices  10.2 us (17%)
  waiting for transfers between devices  9.25 us (15%)
  Pallas kernels  6.32 us (10%)
  local copies, waits for them, and re-layouts  0.7 us (1%)
    all_to_all x1, blocking collectives, body(): lax.all_to_all(packed, 'grp', split_axis=0, concat_axis=0, tiled=True)  17.9 us
    all_to_all x1, blocking collectives, body(): lax.all_to_all(partial, 'blk', split_axis=0, concat_axis=0, tiled=True)  16 us
    all_to_all x1, starting transfers between devices, body(): lax.all_to_all(spread, 'blk', split_axis=0, concat_axis=0, tiled=True)  10.2 us
    all_to_all x1, waiting for transfers between devices, body(): lax.all_to_all(spread, 'blk', split_axis=0, concat_axis=0, tiled=True)  9.25 us
    pallas_call x1, Pallas kernels, body(): pl.pallas_call(attend_kernel, out_shape=jax.ShapeDtypeStruct((devices, RO...  2.2 us
    pallas_call x1, Pallas kernels, body(): pl.pallas_call(fetch_kernel, out_shape=(pltpu.VMEM(pool, bf16), pltpu.VME...  2 us
  transfers between devices with their start and end apart: 1, of which 1 were waited for; matrix products, arithmetic and copies ran while one was open for 0% of the time, Pallas kernels for 3%

profile of v7, /device:TPU:8, one launch (start us, length us, event | category | flops | bytes accessed | tf_op | source)
XLA Modules:
  0.0 60.3 jit_solution(13166035040247593039)
XLA Ops:
  0.0 0.0 copy-start
  0.0 0.7 %copy-done = bf16[192,16]{0,1:T(8,128)(2,1)S(1)} copy-done((bf16[192,16]{0,1:T(8,128)(2,1)S(1)}, bf16[192,16]{0,1:T(8,128)(2,1)}, u32[]{:S(2)}) %copy-start) | copy-done | bytes 6168
  0.7 0.1 pack.1
  0.8 17.9 %all_to_all.15 = bf16[16,8,128]{2,1,0:T(8,128)(2,1)S(1)} all-to-all(bf16[16,8,128]{2,1,0:T(8,128)(2,1)S(1)} %pack.1), channel_id=1, replica_groups=mesh['blk'=32,'grp'=16] {'grp'}, dimensions={0} | all-to-all | bytes 65536 | tf_op jit(solution)/shard_map/all_to_all | solution.py:253
  18.7 1.0 %spread.1 = bf16[32,24,128]{2,1,0:T(8,128)(2,1)} custom-call(bf16[128,128]{1,0:T(8,128)(2,1)S(1)} %bitcast.6), custom_call_target="tpu_custom_call" | custom-call | tf_op jit(solution)/shard_map/spread/pallas_call | solution.py:254
  19.7 10.2 %all-to-all-start.1 = ((bf16[32,24,128]{2,1,0:T(8,128)(2,1)}), bf16[32,24,128]{2,1,0:T(8,128)(2,1)S(1)}, u32[]{:S(2)}, u32[]{:S(2)}) async-start(bf16[32,24,128]{2,1,0:T(8,128)(2,1)} %spread.1), calls=%async_computation.1 | async-start | bytes 393216 | tf_op jit(solution)/shard_map/all_to_all | solution.py:284
  29.9 2.0 %fetch.1 = (bf16[1024,1024]{1,0:T(8,128)(2,1)S(1)}, bf16[1024,512]{1,0:T(8,128)(2,1)S(1)}, f32[24,1024]{1,0:T(8,128)S(1)}) custom-call(s32[1]{0:T(128)} %bitcast.first_ref, s32[1,4]{1,0:T(1,128)} %len_hbm.1, s32[4,128]{1,0:T(4,128)} %bitcast.11, bf16[1024,1024]{1,0:T(8,128)(2,1)} %bitcast.10, bf16[1024,1024]{1,0:T(8,128)(2,1)} %bitcast.8), custom_call_target="tpu_custom_call" | custom-call | flops 1000000000 | bytes 8388608 | tf_op jit(solution)/shard_map/fetch/pallas_call | solution.py:265
  31.9 9.2 %all-to-all-done.1.q_ref = bf16[32,24,128]{2,1,0:T(8,128)(2,1)S(1)} async-done(((bf16[32,24,128]{2,1,0:T(8,128)(2,1)}), bf16[32,24,128]{2,1,0:T(8,128)(2,1)S(1)}, u32[]{:S(2)}, u32[]{:S(2)}) %all-to-all-start.1) | async-done | bytes 196640 | tf_op jit(solution)/shard_map/all_to_all | solution.py:284
  41.1 2.2 %attend.1 = bf16[32,32,128]{2,1,0:T(8,128)(2,1)S(1)} custom-call(f32[24,1024]{1,0:T(8,128)S(1)} %get-tuple-element.8.bias_ref, bf16[32,24,128]{2,1,0:T(8,128)(2,1)S(1)} %all-to-all-done.1.q_ref, bf16[1024,1024]{1,0:T(8,128)(2,1)S(1)} %get-tuple-element.9.k_ref, bf16[1024,512]{1,0:T(8,128)(2,1)S(1)} %get-tuple-element.10.v_ref, bf16[1024,1024]{1,0:T(8,128)(2,1)} %bitcast.9), custom_call_target="tpu_custom_call" | custom-call | tf_op jit(solution)/shard_map/attend/pallas_call | solution.py:286
  43.3 16.0 %all_to_all.16.a_ref = bf16[32,32,128]{2,1,0:T(8,128)(2,1)S(1)} all-to-all(bf16[32,32,128]{2,1,0:T(8,128)(2,1)S(1)} %attend.1), channel_id=1, replica_groups=mesh['blk'=32,'grp'=16] {'blk'}, dimensions={0} | all-to-all | bytes 524288 | tf_op jit(solution)/shard_map/all_to_all | solution.py:302
  59.3 1.0 %combine.1 = bf16[12,256]{1,0:T(8,128)(2,1)} custom-call(bf16[32,32,128]{2,1,0:T(8,128)(2,1)S(1)} %all_to_all.16.a_ref), custom_call_target="tpu_custom_call" | custom-call | tf_op jit(solution)/shard_map/combine/pallas_call | solution.py:303
Async XLA Ops:
  0.0 0.7 %copy-start = (bf16[192,16]{0,1:T(8,128)(2,1)S(1)}, bf16[192,16]{0,1:T(8,128)(2,1)}, u32[]{:S(2)}) copy-start(bf16[192,16]{0,1:T(8,128)(2,1)} %param.5) | copy-start | bytes 18436
  19.7 21.4 %all-to-all-start.1 = ((bf16[32,24,128]{2,1,0:T(8,128)(2,1)}), bf16[32,24,128]{2,1,0:T(8,128)(2,1)S(1)}, u32[]{:S(2)}, u32[]{:S(2)}) async-start(bf16[32,24,128]{2,1,0:T(8,128)(2,1)} %spread.1), calls=%async_computation.1 | async-start | bytes 393216 | tf_op jit(solution)/shard_map/all_to_all | solution.py:284

commit v8 on v7

--- a/solution.py
+++ b/solution.py
@@ -29,6 +29,12 @@
 SCALE = math.log2(math.e) / math.sqrt(DH)
 LN2 = math.log(2.0)
 EMPTY = -1e30
+
+SIDE_X, SIDE_Y = 4, 8
+WALK = [
+    (x if y % 2 == 0 else SIDE_X - 1 - x) * SIDE_Y + y for y in range(SIDE_Y) for x in range(SIDE_X)
+]
+STAND = [WALK.index(b) for b in range(len(WALK))]
 
 VMEM = pl.BlockSpec(memory_space=pltpu.VMEM)
 HBM = pl.BlockSpec(memory_space=pltpu.HBM)
@@ -152,7 +158,7 @@
         return slice(k * DH, (k + 1) * DH)
 
     def scores(k):
-        qk = q_ref[k * SLICES : (k + 1) * SLICES].reshape(rows, DH)
+        qk = jnp.concatenate([q_ref[STAND[k * SLICES + j]] for j in range(SLICES)], axis=0)
         most = None
         for j in range(0, SLOTS * BLOCK, WIDE):
             at = slice(j, j + WIDE)
@@ -187,7 +193,8 @@
             v = late_ref[:, cols(k - EARLY)]
         o = lax.dot_general(p_ref[k % 2], v, nn, preferred_element_type=jnp.float32)
         o = (o * (1.0 / sum_ref[k % 2])).astype(out_ref.dtype)
-        out_ref[k * SLICES : (k + 1) * SLICES, :ROWS, :] = o.reshape(SLICES, ROWS, DH)
+        for j in range(SLICES):
+            out_ref[STAND[k * SLICES + j], :ROWS, :] = o[j * ROWS : (j + 1) * ROWS]
 
     for step in range(KVH + 2):
         if step == LATE:
@@ -212,7 +219,7 @@
         line = high + pltpu.roll(mid, 32, 1) + pltpu.roll(low, 64, 1)
         for k in range(KVH):
             tile = jnp.broadcast_to(line[k : k + 1], (8, LANES))
-            out_ref[k * SLICES + j, ROWS:, :] = tile.astype(out_ref.dtype)
+            out_ref[STAND[k * SLICES + j], ROWS:, :] = tile.astype(out_ref.dtype)
 
 
 def combine_kernel(a_ref, out_ref):
@@ -237,6 +244,12 @@
     out_ref[...] = jnp.concatenate([acc[:TOK], acc[TOK:]], axis=1).astype(out_ref.dtype)
 
 
+def exchange(pieces):
+    return lax.all_to_all(
+        pieces, "blk", split_axis=0, concat_axis=0, tiled=True, axis_index_groups=[WALK]
+    )
+
+
 def body(queries, key_pool, value_pool, lengths, block_table):
     bf16 = jnp.bfloat16
     groups = lax.axis_size("grp")
@@ -281,7 +294,7 @@
         cost_estimate=pl.CostEstimate(flops=10**9, bytes_accessed=8 * 2**20, transcendentals=0),
         name="fetch",
     )(first, in_hbm(lengths), in_hbm(block_table[0]), k_hbm, v_hbm)
-    query_all = lax.all_to_all(spread, "blk", split_axis=0, concat_axis=0, tiled=True)
+    query_all = exchange(spread)
     rows = SLICES * ROWS
     partial = pl.pallas_call(
         attend_kernel,
@@ -299,7 +312,7 @@
         compiler_params=PARAMS,
         name="attend",
     )(bias, query_all, keys, values, v_hbm)
-    collected = lax.all_to_all(partial, "blk", split_axis=0, concat_axis=0, tiled=True)
+    collected = exchange(partial)
     return pl.pallas_call(
         combine_kernel,
         out_shape=jax.ShapeDtypeStruct((TOK, HEADS * DH), bf16),

time: 60.6 us -> 60.6 us (level)
  no operation moved by 1% of the time
where the time goes in v8:
time: 60.6 us; the launch traced here: 60.3 us
  blocking collectives  33.7 us (56%)
  starting transfers between devices  10.2 us (17%)
  waiting for transfers between devices  9.37 us (15%)
  Pallas kernels  6.36 us (10%)
  local copies, waits for them, and re-layouts  0.7 us (1%)
    all_to_all x1, blocking collectives, body(): lax.all_to_all(packed, 'grp', split_axis=0, concat_axis=0, tiled=True)  17.9 us
    all_to_all x1, blocking collectives, exchange(): lax.all_to_all(pieces, 'blk', split_axis=0, concat_axis=0, tiled=True, ax...  15.8 us
    all_to_all x1, starting transfers between devices, exchange(): lax.all_to_all(pieces, 'blk', split_axis=0, concat_axis=0, tiled=True, ax...  10.2 us
    all_to_all x1, waiting for transfers between devices, exchange(): lax.all_to_all(pieces, 'blk', split_axis=0, concat_axis=0, tiled=True, ax...  9.37 us
    pallas_call x1, Pallas kernels, body(): pl.pallas_call(attend_kernel, out_shape=jax.ShapeDtypeStruct((devices, RO...  2.24 us
    pallas_call x1, Pallas kernels, body(): pl.pallas_call(fetch_kernel, out_shape=(pltpu.VMEM(pool, bf16), pltpu.VME...  2 us
  transfers between devices with their start and end apart: 1, of which 1 were waited for; matrix products, arithmetic and copies ran while one was open for 0% of the time, Pallas kernels for 3%

profile of v8, /device:TPU:8, one launch (start us, length us, event | category | flops | bytes accessed | tf_op | source)
XLA Modules:
  0.0 60.3 jit_solution(6937107999030359073)
XLA Ops:
  0.0 0.0 copy-start
  0.0 0.7 %copy-done = bf16[192,16]{0,1:T(8,128)(2,1)S(1)} copy-done((bf16[192,16]{0,1:T(8,128)(2,1)S(1)}, bf16[192,16]{0,1:T(8,128)(2,1)}, u32[]{:S(2)}) %copy-start) | copy-done | bytes 6168
  0.7 0.1 pack.1
  0.8 17.9 %all_to_all.15 = bf16[16,8,128]{2,1,0:T(8,128)(2,1)S(1)} all-to-all(bf16[16,8,128]{2,1,0:T(8,128)(2,1)S(1)} %pack.1), channel_id=1, replica_groups=mesh['blk'=32,'grp'=16] {'grp'}, dimensions={0} | all-to-all | bytes 65536 | tf_op jit(solution)/shard_map/all_to_all | solution.py:266
  18.7 1.0 %spread.1 = bf16[32,24,128]{2,1,0:T(8,128)(2,1)} custom-call(bf16[128,128]{1,0:T(8,128)(2,1)S(1)} %bitcast.6), custom_call_target="tpu_custom_call" | custom-call | tf_op jit(solution)/shard_map/spread/pallas_call | solution.py:267
  19.7 10.2 %all-to-all-start.1 = ((bf16[32,24,128]{2,1,0:T(8,128)(2,1)}), bf16[32,24,128]{2,1,0:T(8,128)(2,1)S(1)}, u32[]{:S(2)}, u32[]{:S(2)}) async-start(bf16[32,24,128]{2,1,0:T(8,128)(2,1)} %spread.1), calls=%async_computation.1 | async-start | bytes 393216 | tf_op jit(solution)/shard_map/all_to_all | solution.py:248
  29.9 2.0 %fetch.1 = (bf16[1024,1024]{1,0:T(8,128)(2,1)S(1)}, bf16[1024,512]{1,0:T(8,128)(2,1)S(1)}, f32[24,1024]{1,0:T(8,128)S(1)}) custom-call(s32[1]{0:T(128)} %bitcast.first_ref, s32[1,4]{1,0:T(1,128)} %len_hbm.1, s32[4,128]{1,0:T(4,128)} %bitcast.11, bf16[1024,1024]{1,0:T(8,128)(2,1)} %bitcast.10, bf16[1024,1024]{1,0:T(8,128)(2,1)} %bitcast.8), custom_call_target="tpu_custom_call" | custom-call | flops 1000000000 | bytes 8388608 | tf_op jit(solution)/shard_map/fetch/pallas_call | solution.py:278
  31.9 9.4 %all-to-all-done.1.q_ref = bf16[32,24,128]{2,1,0:T(8,128)(2,1)S(1)} async-done(((bf16[32,24,128]{2,1,0:T(8,128)(2,1)}), bf16[32,24,128]{2,1,0:T(8,128)(2,1)S(1)}, u32[]{:S(2)}, u32[]{:S(2)}) %all-to-all-start.1) | async-done | bytes 196640 | tf_op jit(solution)/shard_map/all_to_all | solution.py:248
  41.3 2.2 %attend.1 = bf16[32,32,128]{2,1,0:T(8,128)(2,1)S(1)} custom-call(f32[24,1024]{1,0:T(8,128)S(1)} %get-tuple-element.8.bias_ref, bf16[32,24,128]{2,1,0:T(8,128)(2,1)S(1)} %all-to-all-done.1.q_ref, bf16[1024,1024]{1,0:T(8,128)(2,1)S(1)} %get-tuple-element.9.k_ref, bf16[1024,512]{1,0:T(8,128)(2,1)S(1)} %get-tuple-element.10.v_ref, bf16[1024,1024]{1,0:T(8,128)(2,1)} %bitcast.9), custom_call_target="tpu_custom_call" | custom-call | tf_op jit(solution)/shard_map/attend/pallas_call | solution.py:299
  43.5 15.8 %all_to_all.16.a_ref = bf16[32,32,128]{2,1,0:T(8,128)(2,1)S(1)} all-to-all(bf16[32,32,128]{2,1,0:T(8,128)(2,1)S(1)} %attend.1), channel_id=1, replica_groups={{0,128,256,384,400,272,144,16,32,160,288,416,432,304,176,48,64,192,320,..., dimensions={0} | all-to-all | bytes 524288 | tf_op jit(solution)/shard_map/all_to_all | solution.py:248
  59.3 1.0 %combine.1 = bf16[12,256]{1,0:T(8,128)(2,1)} custom-call(bf16[32,32,128]{2,1,0:T(8,128)(2,1)S(1)} %all_to_all.16.a_ref), custom_call_target="tpu_custom_call" | custom-call | tf_op jit(solution)/shard_map/combine/pallas_call | solution.py:316
Async XLA Ops:
  0.0 0.7 %copy-start = (bf16[192,16]{0,1:T(8,128)(2,1)S(1)}, bf16[192,16]{0,1:T(8,128)(2,1)}, u32[]{:S(2)}) copy-start(bf16[192,16]{0,1:T(8,128)(2,1)} %param.5) | copy-start | bytes 18436
  19.7 21.6 %all-to-all-start.1 = ((bf16[32,24,128]{2,1,0:T(8,128)(2,1)}), bf16[32,24,128]{2,1,0:T(8,128)(2,1)S(1)}, u32[]{:S(2)}, u32[]{:S(2)}) async-start(bf16[32,24,128]{2,1,0:T(8,128)(2,1)} %spread.1), calls=%async_computation.1 | async-start | bytes 393216 | tf_op jit(solution)/shard_map/all_to_all | solution.py:248

commit v9 on v8

--- a/solution.py
+++ b/solution.py
@@ -75,20 +75,12 @@
     tok = jnp.where(row >= TOK, row - TOK, row)
     lane = iota((ROWS, LANES), 1)
     nt = (((1,), (1,)), ((), ()))
-    nn = (((1,), (0,)), ((), ()))
-    halves = []
-    for j in range(2):
-        pick = (lane == tok + j * HALF).astype(jnp.bfloat16)
-        halves.append(lax.dot_general(pick, a_ref[...], nt, preferred_element_type=jnp.float32))
-    apart = jnp.concatenate(halves, axis=1).astype(jnp.bfloat16)
-    at = iota((2 * feats, 2 * feats), 0)
-    to = iota((2 * feats, 2 * feats), 1)
-    second = at >= feats
-    at = jnp.where(second, at - feats, at)
-    order = to == (at // HALF_FEATS) * (2 * HALF_FEATS) + at % HALF_FEATS + jnp.where(second, HALF_FEATS, 0)
-    whole = lax.dot_general(
-        apart, order.astype(jnp.bfloat16), nn, preferred_element_type=jnp.float32
-    )
+    tiles = [a_ref[g : g + HALF_FEATS] for g in range(0, feats, HALF_FEATS)]
+    twice = jnp.concatenate([t for t in tiles for _ in range(2)], axis=0)
+    pick = jnp.concatenate([lane == tok, lane == tok + HALF], axis=0).astype(jnp.bfloat16)
+    both = lax.dot_general(pick, twice, nt, preferred_element_type=jnp.float32)
+    odd = (iota((ROWS, 2 * feats), 1) // HALF_FEATS) % 2 == 1
+    whole = jnp.where(odd, both[ROWS:], both[:ROWS])
     rows = jnp.where(row < TOK, whole[:, :LANES], whole[:, LANES:]).astype(out_ref.dtype)
     for b in range(out_ref.shape[0]):
         out_ref[b] = rows

time: 60.6 us -> 60.5 us (level)
  no operation moved by 1% of the time
where the time goes in v9:
time: 60.5 us; the launch traced here: 60.2 us
  blocking collectives  33.7 us (56%)
  starting transfers between devices  10.2 us (17%)
  waiting for transfers between devices  9.37 us (15%)
  Pallas kernels  6.22 us (10%)
  local copies, waits for them, and re-layouts  0.7 us (1%)
    all_to_all x1, blocking collectives, body(): lax.all_to_all(packed, 'grp', split_axis=0, concat_axis=0, tiled=True)  17.9 us
    all_to_all x1, blocking collectives, exchange(): lax.all_to_all(pieces, 'blk', split_axis=0, concat_axis=0, tiled=True, ax...  15.8 us
    all_to_all x1, starting transfers between devices, exchange(): lax.all_to_all(pieces, 'blk', split_axis=0, concat_axis=0, tiled=True, ax...  10.2 us
    all_to_all x1, waiting for transfers between devices, exchange(): lax.all_to_all(pieces, 'blk', split_axis=0, concat_axis=0, tiled=True, ax...  9.37 us
    pallas_call x1, Pallas kernels, body(): pl.pallas_call(attend_kernel, out_shape=jax.ShapeDtypeStruct((devices, RO...  2.25 us
    pallas_call x1, Pallas kernels, body(): pl.pallas_call(fetch_kernel, out_shape=(pltpu.VMEM(pool, bf16), pltpu.VME...  2 us
  transfers between devices with their start and end apart: 1, of which 1 were waited for; matrix products, arithmetic and copies ran while one was open for 0% of the time, Pallas kernels for 3%

profile of v9, /device:TPU:8, one launch (start us, length us, event | category | flops | bytes accessed | tf_op | source)
XLA Modules:
  0.0 60.2 jit_solution(1421536089321482293)
XLA Ops:
  0.0 0.0 copy-start
  0.0 0.7 %copy-done = bf16[192,16]{0,1:T(8,128)(2,1)S(1)} copy-done((bf16[192,16]{0,1:T(8,128)(2,1)S(1)}, bf16[192,16]{0,1:T(8,128)(2,1)}, u32[]{:S(2)}) %copy-start) | copy-done | bytes 6168
  0.7 0.1 pack.1
  0.8 17.9 %all_to_all.15 = bf16[16,8,128]{2,1,0:T(8,128)(2,1)S(1)} all-to-all(bf16[16,8,128]{2,1,0:T(8,128)(2,1)S(1)} %pack.1), channel_id=1, replica_groups=mesh['blk'=32,'grp'=16] {'grp'}, dimensions={0} | all-to-all | bytes 65536 | tf_op jit(solution)/shard_map/all_to_all | solution.py:258
  18.7 0.8 %spread.1 = bf16[32,24,128]{2,1,0:T(8,128)(2,1)} custom-call(bf16[128,128]{1,0:T(8,128)(2,1)S(1)} %bitcast.6), custom_call_target="tpu_custom_call" | custom-call | tf_op jit(solution)/shard_map/spread/pallas_call | solution.py:259
  19.6 10.2 %all-to-all-start.1 = ((bf16[32,24,128]{2,1,0:T(8,128)(2,1)}), bf16[32,24,128]{2,1,0:T(8,128)(2,1)S(1)}, u32[]{:S(2)}, u32[]{:S(2)}) async-start(bf16[32,24,128]{2,1,0:T(8,128)(2,1)} %spread.1), calls=%async_computation.1 | async-start | bytes 393216 | tf_op jit(solution)/shard_map/all_to_all | solution.py:240
  29.7 2.0 %fetch.1 = (bf16[1024,1024]{1,0:T(8,128)(2,1)S(1)}, bf16[1024,512]{1,0:T(8,128)(2,1)S(1)}, f32[24,1024]{1,0:T(8,128)S(1)}) custom-call(s32[1]{0:T(128)} %bitcast.first_ref, s32[1,4]{1,0:T(1,128)} %len_hbm.1, s32[4,128]{1,0:T(4,128)} %bitcast.11, bf16[1024,1024]{1,0:T(8,128)(2,1)} %bitcast.10, bf16[1024,1024]{1,0:T(8,128)(2,1)} %bitcast.8), custom_call_target="tpu_custom_call" | custom-call | flops 1000000000 | bytes 8388608 | tf_op jit(solution)/shard_map/fetch/pallas_call | solution.py:270
  31.7 9.4 %all-to-all-done.1.q_ref = bf16[32,24,128]{2,1,0:T(8,128)(2,1)S(1)} async-done(((bf16[32,24,128]{2,1,0:T(8,128)(2,1)}), bf16[32,24,128]{2,1,0:T(8,128)(2,1)S(1)}, u32[]{:S(2)}, u32[]{:S(2)}) %all-to-all-start.1) | async-done | bytes 196640 | tf_op jit(solution)/shard_map/all_to_all | solution.py:240
  41.1 2.2 %attend.1 = bf16[32,32,128]{2,1,0:T(8,128)(2,1)S(1)} custom-call(f32[24,1024]{1,0:T(8,128)S(1)} %get-tuple-element.8.bias_ref, bf16[32,24,128]{2,1,0:T(8,128)(2,1)S(1)} %all-to-all-done.1.q_ref, bf16[1024,1024]{1,0:T(8,128)(2,1)S(1)} %get-tuple-element.9.k_ref, bf16[1024,512]{1,0:T(8,128)(2,1)S(1)} %get-tuple-element.10.v_ref, bf16[1024,1024]{1,0:T(8,128)(2,1)} %bitcast.9), custom_call_target="tpu_custom_call" | custom-call | tf_op jit(solution)/shard_map/attend/pallas_call | solution.py:291
  43.4 15.8 %all_to_all.16.a_ref = bf16[32,32,128]{2,1,0:T(8,128)(2,1)S(1)} all-to-all(bf16[32,32,128]{2,1,0:T(8,128)(2,1)S(1)} %attend.1), channel_id=1, replica_groups={{0,128,256,384,400,272,144,16,32,160,288,416,432,304,176,48,64,192,320,..., dimensions={0} | all-to-all | bytes 524288 | tf_op jit(solution)/shard_map/all_to_all | solution.py:240
  59.1 1.0 %combine.1 = bf16[12,256]{1,0:T(8,128)(2,1)} custom-call(bf16[32,32,128]{2,1,0:T(8,128)(2,1)S(1)} %all_to_all.16.a_ref), custom_call_target="tpu_custom_call" | custom-call | tf_op jit(solution)/shard_map/combine/pallas_call | solution.py:308
Async XLA Ops:
  0.0 0.7 %copy-start = (bf16[192,16]{0,1:T(8,128)(2,1)S(1)}, bf16[192,16]{0,1:T(8,128)(2,1)}, u32[]{:S(2)}) copy-start(bf16[192,16]{0,1:T(8,128)(2,1)} %param.5) | copy-start | bytes 18436
  19.6 21.6 %all-to-all-start.1 = ((bf16[32,24,128]{2,1,0:T(8,128)(2,1)}), bf16[32,24,128]{2,1,0:T(8,128)(2,1)S(1)}, u32[]{:S(2)}, u32[]{:S(2)}) async-start(bf16[32,24,128]{2,1,0:T(8,128)(2,1)} %spread.1), calls=%async_computation.1 | async-start | bytes 393216 | tf_op jit(solution)/shard_map/all_to_all | solution.py:240

commit v10 on v9

--- a/solution.py
+++ b/solution.py
@@ -20,9 +20,6 @@
 WIDE = 256
 CHUNK = 16
 BLOCK = 128
-FETCHES = 8
-LATE = 6
-EARLY = 4
 LANES = 128
 HALF_FEATS = 8
 HALF = 16
@@ -41,6 +38,7 @@
 SMEM = pl.BlockSpec(memory_space=pltpu.SMEM)
 
 
+LONG = pl.CostEstimate(flops=10**10, bytes_accessed=10**8, transcendentals=10**6)
 PARAMS = pltpu.CompilerParams(vmem_limit_bytes=16 * 1024 * 1024)
 
 
@@ -52,7 +50,18 @@
     return lax.broadcasted_iota(jnp.int32, shape, dim)
 
 
-def pack_kernel(q_ref, out_ref):
+def pack_kernel(
+    first_ref, len_hbm, table_hbm, q_hbm, out_ref, bias_ref, len_ref, table_ref, q_ref, sems
+):
+    copies = [
+        pltpu.make_async_copy(q_hbm, q_ref, sems.at[0]),
+        pltpu.make_async_copy(table_hbm, table_ref, sems.at[1]),
+        pltpu.make_async_copy(len_hbm, len_ref, sems.at[2]),
+    ]
+    for c in copies:
+        c.start()
+    for c in copies:
+        c.wait()
     groups, feats, _ = out_ref.shape
     q = q_ref[...].astype(jnp.float32)
     lane = iota((feats, LANES), 1)
@@ -67,6 +76,22 @@
         high = turned(wide[feats:], HALF - g * TOK)
         both = jnp.where(lane < TOK, low, jnp.where((lane >= HALF) & (lane < HALF + TOK), high, 0.0))
         out_ref[g] = both.astype(out_ref.dtype)
+
+    lane4 = iota((SEQS, LANES), 1)
+    sub4 = iota((SEQS, LANES), 0)
+    lens = jnp.zeros((SEQS, LANES), jnp.int32)
+    for q in range(SEQS):
+        lens = jnp.where(sub4 == q, len_ref[0, q], lens)
+    local = jnp.where(lane4 < lens, table_ref[...] - first_ref[0], -1)
+    row = iota((ROWS, LANES), 0)
+    seq = jnp.where(row >= TOK, row - TOK, row) // STEPS
+    for s in range(SLOTS):
+        hit = jnp.max((local == s).astype(jnp.float32), axis=1, keepdims=True)
+        off = jnp.broadcast_to(jnp.where(hit > 0.0, 0.0, EMPTY), (SEQS, LANES))
+        b = jnp.broadcast_to(off[0:1], (ROWS, LANES))
+        for q in range(1, SEQS):
+            b = jnp.where(seq == q, off[q : q + 1], b)
+        bias_ref[:, s * BLOCK : (s + 1) * BLOCK] = b
 
 
 def spread_kernel(a_ref, out_ref):
@@ -86,60 +111,7 @@
         out_ref[b] = rows
 
 
-def fetch_kernel(
-    first_ref, len_hbm, table_hbm, k_hbm, v_hbm,
-    k_ref, v_ref, bias_ref, len_ref, table_ref, sems, small,
-):
-    rows = k_ref.shape[0] // FETCHES
-    copies = []
-    for i in range(FETCHES):
-        at = pl.ds(i * rows, rows)
-        copies.append(pltpu.make_async_copy(k_hbm.at[at], k_ref.at[at], sems.at[0, i]))
-        copies.append(
-            pltpu.make_async_copy(v_hbm.at[at, pl.ds(0, EARLY * DH)], v_ref.at[at], sems.at[1, i])
-        )
-    facts = [
-        pltpu.make_async_copy(table_hbm, table_ref, small.at[0]),
-        pltpu.make_async_copy(len_hbm, len_ref, small.at[1]),
-    ]
-    for c in facts + copies:
-        c.start()
-    for c in facts:
-        c.wait()
-    lane4 = iota((SEQS, LANES), 1)
-    sub4 = iota((SEQS, LANES), 0)
-    lens = jnp.zeros((SEQS, LANES), jnp.int32)
-    for q in range(SEQS):
-        lens = jnp.where(sub4 == q, len_ref[0, q], lens)
-    local = jnp.where(lane4 < lens, table_ref[...] - first_ref[0], -1)
-    row = iota((ROWS, LANES), 0)
-    seq = jnp.where(row >= TOK, row - TOK, row) // STEPS
-    for s in range(SLOTS):
-        hit = jnp.max((local == s).astype(jnp.float32), axis=1, keepdims=True)
-        off = jnp.broadcast_to(jnp.where(hit > 0.0, 0.0, EMPTY), (SEQS, LANES))
-        b = jnp.broadcast_to(off[0:1], (ROWS, LANES))
-        for q in range(1, SEQS):
-            b = jnp.where(seq == q, off[q : q + 1], b)
-        bias_ref[:, s * BLOCK : (s + 1) * BLOCK] = b
-    for c in copies:
-        c.wait()
-
-
-def attend_kernel(
-    bias_ref, q_ref, k_ref, v_ref, v_hbm, out_ref, late_ref, s_ref, p_ref, top_ref, sum_ref, sems
-):
-    def late(k):
-        return pltpu.make_async_copy(
-            v_hbm.at[:, pl.ds(pl.multiple_of((EARLY + k) * DH, DH), DH)],
-            late_ref.at[:, pl.ds(pl.multiple_of(k * DH, DH), DH)],
-            sems.at[k],
-        )
-
-    def send_for(k, carry):
-        late(k).start()
-        return carry
-
-    lax.fori_loop(0, KVH - EARLY, send_for, 0)
+def attend_kernel(bias_ref, q_ref, k_ref, v_ref, out_ref, s_ref, p_ref, top_ref, sum_ref):
     rows = SLICES * ROWS
     lane = iota((rows, LANES), 1)
     lse = jnp.zeros((rows, LANES), jnp.float32)
@@ -179,19 +151,14 @@
         return jnp.where(lane == k, top_ref[k] * SCALE + jnp.log2(sum_ref[k % 2]), lse)
 
     def values(k):
-        if k < EARLY:
-            v = v_ref[:, cols(k)]
-        else:
-            v = late_ref[:, cols(k - EARLY)]
-        o = lax.dot_general(p_ref[k % 2], v, nn, preferred_element_type=jnp.float32)
+        o = lax.dot_general(
+            p_ref[k % 2], v_ref[:, cols(k)], nn, preferred_element_type=jnp.float32
+        )
         o = (o * (1.0 / sum_ref[k % 2])).astype(out_ref.dtype)
         for j in range(SLICES):
             out_ref[STAND[k * SLICES + j], :ROWS, :] = o[j * ROWS : (j + 1) * ROWS]
 
     for step in range(KVH + 2):
-        if step == LATE:
-            for k in range(KVH - EARLY):
-                late(k).wait()
         if step < KVH:
             scores(step)
         if 0 <= step - 1 < KVH:
@@ -247,14 +214,24 @@
     groups = lax.axis_size("grp")
     devices = lax.axis_size("blk")
     first = (lax.axis_index("blk") * SLOTS).astype(jnp.int32).reshape(1)
-    packed = pl.pallas_call(
+    packed, bias = pl.pallas_call(
         pack_kernel,
-        out_shape=jax.ShapeDtypeStruct((groups, HALF_FEATS, LANES), bf16),
-        in_specs=[VMEM],
-        out_specs=VMEM,
-        compiler_params=PARAMS,
+        out_shape=(
+            jax.ShapeDtypeStruct((groups, HALF_FEATS, LANES), bf16),
+            jax.ShapeDtypeStruct((ROWS, SLOTS * BLOCK), jnp.float32),
+        ),
+        in_specs=[SMEM, HBM, HBM, HBM],
+        out_specs=(VMEM, VMEM),
+        scratch_shapes=[
+            pltpu.SMEM(lengths.shape, jnp.int32),
+            pltpu.VMEM(block_table.shape[1:], jnp.int32),
+            pltpu.VMEM(queries.shape[::-1], bf16),
+            pltpu.SemaphoreType.DMA((3,)),
+        ],
+        compiler_params=PARAMS,
+        cost_estimate=LONG,
         name="pack",
-    )(queries.T)
+    )(first, in_hbm(lengths), in_hbm(block_table[0]), in_hbm(queries.T))
     arrived = lax.all_to_all(packed, "grp", split_axis=0, concat_axis=0, tiled=True)
     spread = pl.pallas_call(
         spread_kernel,
@@ -262,48 +239,27 @@
         in_specs=[VMEM],
         out_specs=VMEM,
         compiler_params=PARAMS,
+        cost_estimate=LONG,
         name="spread",
     )(arrived.reshape(groups * HALF_FEATS, LANES))
-    pool = (SLOTS * BLOCK, KVH * DH)
-    k_hbm = in_hbm(key_pool.reshape(pool))
-    v_hbm = in_hbm(value_pool.reshape(pool))
-    keys, values, bias = pl.pallas_call(
-        fetch_kernel,
-        out_shape=(
-            pltpu.VMEM(pool, bf16),
-            pltpu.VMEM((pool[0], EARLY * DH), bf16),
-            pltpu.VMEM((ROWS, pool[0]), jnp.float32),
-        ),
-        in_specs=[SMEM, HBM, HBM, HBM, HBM],
-        out_specs=(VMEM,) * 3,
-        scratch_shapes=[
-            pltpu.SMEM(lengths.shape, jnp.int32),
-            pltpu.VMEM(block_table.shape[1:], jnp.int32),
-            pltpu.SemaphoreType.DMA((2, FETCHES)),
-            pltpu.SemaphoreType.DMA((2,)),
-        ],
-        compiler_params=PARAMS,
-        cost_estimate=pl.CostEstimate(flops=10**9, bytes_accessed=8 * 2**20, transcendentals=0),
-        name="fetch",
-    )(first, in_hbm(lengths), in_hbm(block_table[0]), k_hbm, v_hbm)
     query_all = exchange(spread)
     rows = SLICES * ROWS
+    pool = (SLOTS * BLOCK, KVH * DH)
     partial = pl.pallas_call(
         attend_kernel,
         out_shape=jax.ShapeDtypeStruct((devices, ROWS + 8, LANES), bf16),
-        in_specs=[VMEM] * 4 + [HBM],
+        in_specs=[VMEM] * 4,
         out_specs=VMEM,
         scratch_shapes=[
-            pltpu.VMEM((pool[0], (KVH - EARLY) * DH), bf16),
             pltpu.VMEM((2, rows, pool[0]), jnp.float32),
             pltpu.VMEM((2, rows, pool[0]), bf16),
             pltpu.VMEM((KVH, rows, LANES), jnp.float32),
             pltpu.VMEM((2, rows, LANES), jnp.float32),
-            pltpu.SemaphoreType.DMA((KVH - EARLY,)),
         ],
         compiler_params=PARAMS,
+        cost_estimate=LONG,
         name="attend",
-    )(bias, query_all, keys, values, v_hbm)
+    )(bias, query_all, key_pool.reshape(pool), value_pool.reshape(pool))
     collected = exchange(partial)
     return pl.pallas_call(
         combine_kernel,

time: 60.5 us -> 60.1 us (level)
  blocking collectives: 33.7 us -> 55.3 us
  starting transfers between devices: 10.2 us -> 0 us
  waiting for transfers between devices: 9.37 us -> 0 us
  Pallas kernels: 6.22 us -> 4.5 us
  local copies, waits for them, and re-layouts: 0.7 us -> 0.01 us
    all_to_all x1 -> x2, blocking collectives: 15.8 us -> 37.4 us  [exchange(): lax.all_to_all(pieces, 'blk', split_axis=0, concat_axis=0, tiled=True, ax...]
    all_to_all x1 -> x0, starting transfers between devices: 10.2 us -> none  [exchange(): lax.all_to_all(pieces, 'blk', split_axis=0, concat_axis=0, tiled=True, ax...]
    all_to_all x1 -> x0, waiting for transfers between devices: 9.37 us -> none  [exchange(): lax.all_to_all(pieces, 'blk', split_axis=0, concat_axis=0, tiled=True, ax...]
    pallas_call x2 -> x1, Pallas kernels: 2.1 us -> 0.96 us  [body(): pl.pallas_call(pack_kernel, out_shape=(jax.ShapeDtypeStruct((groups, HALF...]
    unnamed x2 -> x4, local copies, waits for them, and re-layouts: 0.7 us -> 0.01 us
    pallas_call x1, Pallas kernels: 0.84 us -> 0.17 us  [body(): pl.pallas_call(spread_kernel, out_shape=jax.ShapeDtypeStruct((devices, RO...]
  transfers between devices with their start and end apart: 1 -> 0, of which waited for: 1 -> 0; matrix products, arithmetic and copies ran while one was open for 0% -> 0% of each run, Pallas kernels for 3% -> 0%
where the time goes in v10:
time: 60.1 us; the launch traced here: 59.8 us
  blocking collectives  55.3 us (92%)
  Pallas kernels  4.5 us (7%)
    all_to_all x2, blocking collectives, exchange(): lax.all_to_all(pieces, 'blk', split_axis=0, concat_axis=0, tiled=True, ax...  37.4 us
    all_to_all x1, blocking collectives, body(): lax.all_to_all(packed, 'grp', split_axis=0, concat_axis=0, tiled=True)  17.9 us
    pallas_call x1, Pallas kernels, body(): pl.pallas_call(attend_kernel, out_shape=jax.ShapeDtypeStruct((devices, RO...  2.34 us

profile of v10, /device:TPU:8, one launch (start us, length us, event | category | flops | bytes accessed | tf_op | source)
XLA Modules:
  0.0 59.8 jit_solution(12940835840870556590)
XLA Ops:
  0.0 1.0 %pack.1 = (bf16[16,8,128]{2,1,0:T(8,128)(2,1)S(1)}, f32[24,1024]{1,0:T(8,128)S(1)}) custom-call(s32[1]{0:T(128)} %bitcast.first_ref, s32[1,4]{1,0:T(1,128)} %len_hbm.1, s32[4,128]{1,0:T(4,128)} %bitcast.10, bf16[16,192]{1,0:T(8,128)(2,1)} %bitcast.9), custom_call_target="tpu_custom_call" | custom-call | flops 10000000000 | bytes 100000000 | tf_op jit(solution)/shard_map/pack/pallas_call | solution.py:217
  1.0 17.9 %all_to_all.15 = bf16[16,8,128]{2,1,0:T(8,128)(2,1)S(1)} all-to-all(bf16[16,8,128]{2,1,0:T(8,128)(2,1)S(1)} %get-tuple-element.8), channel_id=1, replica_groups=mesh['blk'=32,'grp'=16] {'grp'}, dimensions={0} | all-to-all | bytes 65536 | tf_op jit(solution)/shard_map/all_to_all | solution.py:235
  18.9 0.0 copy-start
  18.9 0.0 copy-start.1
  18.9 0.2 spread.1
  19.1 21.6 %all_to_all.16.q_ref = bf16[32,24,128]{2,1,0:T(8,128)(2,1)S(1)} all-to-all(bf16[32,24,128]{2,1,0:T(8,128)(2,1)S(1)} %spread.1), channel_id=1, replica_groups={{0,128,256,384,400,272,144,16,32,160,288,416,432,304,176,48,64,192,320,..., dimensions={0} | all-to-all | bytes 393216 | tf_op jit(solution)/shard_map/all_to_all | solution.py:207
  40.7 0.0 copy-done
  40.7 0.0 copy-done.1
  40.7 2.3 %attend.1 = bf16[32,32,128]{2,1,0:T(8,128)(2,1)S(1)} custom-call(f32[24,1024]{1,0:T(8,128)S(1)} %get-tuple-element.7.bias_ref, bf16[32,24,128]{2,1,0:T(8,128)(2,1)S(1)} %all_to_all.16.q_ref, bf16[1024,1024]{1,0:T(8,128)(2,1)S(1)} %bitcast.7, bf16[1024,1024]{1,0:T(8,128)(2,1)S(1)} %bitcast.8), custom_call_target="tpu_custom_call" | custom-call | flops 10000000000 | bytes 100000000 | tf_op jit(solution)/shard_map/attend/pallas_call | solution.py:248
  43.0 15.8 %all_to_all.17.a_ref = bf16[32,32,128]{2,1,0:T(8,128)(2,1)S(1)} all-to-all(bf16[32,32,128]{2,1,0:T(8,128)(2,1)S(1)} %attend.1), channel_id=1, replica_groups={{0,128,256,384,400,272,144,16,32,160,288,416,432,304,176,48,64,192,320,..., dimensions={0} | all-to-all | bytes 524288 | tf_op jit(solution)/shard_map/all_to_all | solution.py:207
  58.8 1.0 %combine.1 = bf16[12,256]{1,0:T(8,128)(2,1)} custom-call(bf16[32,32,128]{2,1,0:T(8,128)(2,1)S(1)} %all_to_all.17.a_ref), custom_call_target="tpu_custom_call" | custom-call | tf_op jit(solution)/shard_map/combine/pallas_call | solution.py:264
Async XLA Ops:
  18.9 21.8 %copy-start = (bf16[1,8,128,1024]{3,2,1,0:T(8,128)(2,1)S(1)}, bf16[1,8,128,1024]{3,2,1,0:T(8,128)(2,1)}, u32[]{:S(2)}) copy-start(bf16[1,8,128,1024]{3,2,1,0:T(8,128)(2,1)} %param.6) | copy-start | bytes 6291460
  18.9 21.8 %copy-start.1 = (bf16[1,8,128,1024]{3,2,1,0:T(8,128)(2,1)S(1)}, bf16[1,8,128,1024]{3,2,1,0:T(8,128)(2,1)}, u32[]{:S(2)}) copy-start(bf16[1,8,128,1024]{3,2,1,0:T(8,128)(2,1)} %param.7) | copy-start | bytes 6291460

commit v11 on v10

--- a/solution.py
+++ b/solution.py
@@ -35,7 +35,6 @@
 
 VMEM = pl.BlockSpec(memory_space=pltpu.VMEM)
 HBM = pl.BlockSpec(memory_space=pltpu.HBM)
-SMEM = pl.BlockSpec(memory_space=pltpu.SMEM)
 
 
 LONG = pl.CostEstimate(flops=10**10, bytes_accessed=10**8, transcendentals=10**6)
@@ -51,7 +50,7 @@
 
 
 def pack_kernel(
-    first_ref, len_hbm, table_hbm, q_hbm, out_ref, bias_ref, len_ref, table_ref, q_ref, sems
+    len_hbm, table_hbm, q_hbm, out_ref, bias_ref, len_ref, table_ref, q_ref, sems
 ):
     copies = [
         pltpu.make_async_copy(q_hbm, q_ref, sems.at[0]),
@@ -82,7 +81,7 @@
     lens = jnp.zeros((SEQS, LANES), jnp.int32)
     for q in range(SEQS):
         lens = jnp.where(sub4 == q, len_ref[0, q], lens)
-    local = jnp.where(lane4 < lens, table_ref[...] - first_ref[0], -1)
+    local = jnp.where(lane4 < lens, table_ref[...] - lax.axis_index("blk") * SLOTS, -1)
     row = iota((ROWS, LANES), 0)
     seq = jnp.where(row >= TOK, row - TOK, row) // STEPS
     for s in range(SLOTS):
@@ -213,14 +212,13 @@
     bf16 = jnp.bfloat16
     groups = lax.axis_size("grp")
     devices = lax.axis_size("blk")
-    first = (lax.axis_index("blk") * SLOTS).astype(jnp.int32).reshape(1)
     packed, bias = pl.pallas_call(
         pack_kernel,
         out_shape=(
             jax.ShapeDtypeStruct((groups, HALF_FEATS, LANES), bf16),
             jax.ShapeDtypeStruct((ROWS, SLOTS * BLOCK), jnp.float32),
         ),
-        in_specs=[SMEM, HBM, HBM, HBM],
+        in_specs=[HBM, HBM, HBM],
         out_specs=(VMEM, VMEM),
         scratch_shapes=[
             pltpu.SMEM(lengths.shape, jnp.int32),
@@ -231,7 +229,7 @@
         compiler_params=PARAMS,
         cost_estimate=LONG,
         name="pack",
-    )(first, in_hbm(lengths), in_hbm(block_table[0]), in_hbm(queries.T))
+    )(in_hbm(lengths), in_hbm(block_table[0]), in_hbm(queries.T))
     arrived = lax.all_to_all(packed, "grp", split_axis=0, concat_axis=0, tiled=True)
     spread = pl.pallas_call(
         spread_kernel,

time: 60.1 us -> 60.1 us (level)
  no operation moved by 1% of the time
where the time goes in v11:
time: 60.1 us; the launch traced here: 59.8 us
  blocking collectives  55.3 us (92%)
  Pallas kernels  4.5 us (7%)
    all_to_all x2, blocking collectives, exchange(): lax.all_to_all(pieces, 'blk', split_axis=0, concat_axis=0, tiled=True, ax...  37.4 us
    all_to_all x1, blocking collectives, body(): lax.all_to_all(packed, 'grp', split_axis=0, concat_axis=0, tiled=True)  17.9 us
    pallas_call x1, Pallas kernels, body(): pl.pallas_call(attend_kernel, out_shape=jax.ShapeDtypeStruct((devices, RO...  2.34 us

profile of v11, /device:TPU:8, one launch (start us, length us, event | category | flops | bytes accessed | tf_op | source)
XLA Modules:
  0.0 59.8 jit_solution(14436366075238930198)
XLA Ops:
  0.0 1.0 %pack.1 = (bf16[16,8,128]{2,1,0:T(8,128)(2,1)S(1)}, f32[24,1024]{1,0:T(8,128)S(1)}) custom-call(s32[1,4]{1,0:T(1,128)} %len_hbm.1, s32[4,128]{1,0:T(4,128)} %bitcast.9, bf16[16,192]{1,0:T(8,128)(2,1)} %bitcast.8), custom_call_target="tpu_custom_call" | custom-call | flops 10000000000 | bytes 100000000 | tf_op jit(solution)/shard_map/pack/pallas_call | solution.py:215
  1.0 17.9 %all_to_all.15 = bf16[16,8,128]{2,1,0:T(8,128)(2,1)S(1)} all-to-all(bf16[16,8,128]{2,1,0:T(8,128)(2,1)S(1)} %get-tuple-element.8), channel_id=1, replica_groups=mesh['blk'=32,'grp'=16] {'grp'}, dimensions={0} | all-to-all | bytes 65536 | tf_op jit(solution)/shard_map/all_to_all | solution.py:233
  18.9 0.0 copy-start
  18.9 0.0 copy-start.1
  18.9 0.2 spread.1
  19.1 21.6 %all_to_all.16.q_ref = bf16[32,24,128]{2,1,0:T(8,128)(2,1)S(1)} all-to-all(bf16[32,24,128]{2,1,0:T(8,128)(2,1)S(1)} %spread.1), channel_id=1, replica_groups={{0,128,256,384,400,272,144,16,32,160,288,416,432,304,176,48,64,192,320,..., dimensions={0} | all-to-all | bytes 393216 | tf_op jit(solution)/shard_map/all_to_all | solution.py:206
  40.7 0.0 copy-done
  40.7 0.0 copy-done.1
  40.7 2.3 %attend.1 = bf16[32,32,128]{2,1,0:T(8,128)(2,1)S(1)} custom-call(f32[24,1024]{1,0:T(8,128)S(1)} %get-tuple-element.7.bias_ref, bf16[32,24,128]{2,1,0:T(8,128)(2,1)S(1)} %all_to_all.16.q_ref, bf16[1024,1024]{1,0:T(8,128)(2,1)S(1)} %bitcast.6, bf16[1024,1024]{1,0:T(8,128)(2,1)S(1)} %bitcast.7), custom_call_target="tpu_custom_call" | custom-call | flops 10000000000 | bytes 100000000 | tf_op jit(solution)/shard_map/attend/pallas_call | solution.py:246
  43.0 15.8 %all_to_all.17.a_ref = bf16[32,32,128]{2,1,0:T(8,128)(2,1)S(1)} all-to-all(bf16[32,32,128]{2,1,0:T(8,128)(2,1)S(1)} %attend.1), channel_id=1, replica_groups={{0,128,256,384,400,272,144,16,32,160,288,416,432,304,176,48,64,192,320,..., dimensions={0} | all-to-all | bytes 524288 | tf_op jit(solution)/shard_map/all_to_all | solution.py:206
  58.8 1.0 %combine.1 = bf16[12,256]{1,0:T(8,128)(2,1)} custom-call(bf16[32,32,128]{2,1,0:T(8,128)(2,1)S(1)} %all_to_all.17.a_ref), custom_call_target="tpu_custom_call" | custom-call | tf_op jit(solution)/shard_map/combine/pallas_call | solution.py:262
Async XLA Ops:
  18.9 21.8 %copy-start = (bf16[1,8,128,1024]{3,2,1,0:T(8,128)(2,1)S(1)}, bf16[1,8,128,1024]{3,2,1,0:T(8,128)(2,1)}, u32[]{:S(2)}) copy-start(bf16[1,8,128,1024]{3,2,1,0:T(8,128)(2,1)} %param.6) | copy-start | bytes 6291460
  18.9 21.8 %copy-start.1 = (bf16[1,8,128,1024]{3,2,1,0:T(8,128)(2,1)S(1)}, bf16[1,8,128,1024]{3,2,1,0:T(8,128)(2,1)}, u32[]{:S(2)}) copy-start(bf16[1,8,128,1024]{3,2,1,0:T(8,128)(2,1)} %param.7) | copy-start | bytes 6291460

commit v12 on v10

--- a/solution.py
+++ b/solution.py
@@ -122,7 +122,7 @@
         return slice(k * DH, (k + 1) * DH)
 
     def scores(k):
-        qk = jnp.concatenate([q_ref[STAND[k * SLICES + j]] for j in range(SLICES)], axis=0)
+        qk = q_ref[k * SLICES : (k + 1) * SLICES].reshape(rows, DH)
         most = None
         for j in range(0, SLOTS * BLOCK, WIDE):
             at = slice(j, j + WIDE)
@@ -242,7 +242,7 @@
         cost_estimate=LONG,
         name="spread",
     )(arrived.reshape(groups * HALF_FEATS, LANES))
-    query_all = exchange(spread)
+    query_all = lax.all_to_all(spread, "blk", split_axis=0, concat_axis=0, tiled=True)
     rows = SLICES * ROWS
     pool = (SLOTS * BLOCK, KVH * DH)
     partial = pl.pallas_call(

time: 60.1 us -> 60.3 us (level)
    all_to_all x0 -> x1, blocking collectives: none -> 21.5 us  [body(): lax.all_to_all(spread, 'blk', split_axis=0, concat_axis=0, tiled=True)]
    all_to_all x2 -> x1, blocking collectives: 37.4 us -> 16.1 us  [exchange(): lax.all_to_all(pieces, 'blk', split_axis=0, concat_axis=0, tiled=True, ax...]
where the time goes in v12:
time: 60.3 us; the launch traced here: 60 us
  blocking collectives  55.5 us (92%)
  Pallas kernels  4.52 us (7%)
    all_to_all x1, blocking collectives, body(): lax.all_to_all(spread, 'blk', split_axis=0, concat_axis=0, tiled=True)  21.5 us
    all_to_all x1, blocking collectives, body(): lax.all_to_all(packed, 'grp', split_axis=0, concat_axis=0, tiled=True)  17.9 us
    all_to_all x1, blocking collectives, exchange(): lax.all_to_all(pieces, 'blk', split_axis=0, concat_axis=0, tiled=True, ax...  16.1 us
    pallas_call x1, Pallas kernels, body(): pl.pallas_call(attend_kernel, out_shape=jax.ShapeDtypeStruct((devices, RO...  2.36 us

profile of v12, /device:TPU:8, one launch (start us, length us, event | category | flops | bytes accessed | tf_op | source)
XLA Modules:
  0.0 60.0 jit_solution(11173418404794453898)
XLA Ops:
  0.0 1.0 %pack.1 = (bf16[16,8,128]{2,1,0:T(8,128)(2,1)S(1)}, f32[24,1024]{1,0:T(8,128)S(1)}) custom-call(s32[1]{0:T(128)} %bitcast.first_ref, s32[1,4]{1,0:T(1,128)} %len_hbm.1, s32[4,128]{1,0:T(4,128)} %bitcast.10, bf16[16,192]{1,0:T(8,128)(2,1)} %bitcast.9), custom_call_target="tpu_custom_call" | custom-call | flops 10000000000 | bytes 100000000 | tf_op jit(solution)/shard_map/pack/pallas_call | solution.py:217
  1.0 17.9 %all_to_all.15 = bf16[16,8,128]{2,1,0:T(8,128)(2,1)S(1)} all-to-all(bf16[16,8,128]{2,1,0:T(8,128)(2,1)S(1)} %get-tuple-element.8), channel_id=1, replica_groups=mesh['blk'=32,'grp'=16] {'grp'}, dimensions={0} | all-to-all | bytes 65536 | tf_op jit(solution)/shard_map/all_to_all | solution.py:235
  18.9 0.0 copy-start
  18.9 0.0 copy-start.1
  18.9 0.2 spread.1
  19.1 21.5 %all_to_all.16.q_ref = bf16[32,24,128]{2,1,0:T(8,128)(2,1)S(1)} all-to-all(bf16[32,24,128]{2,1,0:T(8,128)(2,1)S(1)} %spread.1), channel_id=1, replica_groups=mesh['blk'=32,'grp'=16] {'blk'}, dimensions={0} | all-to-all | bytes 393216 | tf_op jit(solution)/shard_map/all_to_all | solution.py:245
  40.5 0.0 copy-done
  40.5 0.0 copy-done.1
  40.5 2.4 %attend.1 = bf16[32,32,128]{2,1,0:T(8,128)(2,1)S(1)} custom-call(f32[24,1024]{1,0:T(8,128)S(1)} %get-tuple-element.7.bias_ref, bf16[32,24,128]{2,1,0:T(8,128)(2,1)S(1)} %all_to_all.16.q_ref, bf16[1024,1024]{1,0:T(8,128)(2,1)S(1)} %bitcast.7, bf16[1024,1024]{1,0:T(8,128)(2,1)S(1)} %bitcast.8), custom_call_target="tpu_custom_call" | custom-call | flops 10000000000 | bytes 100000000 | tf_op jit(solution)/shard_map/attend/pallas_call | solution.py:248
  42.9 16.1 %all_to_all.17.a_ref = bf16[32,32,128]{2,1,0:T(8,128)(2,1)S(1)} all-to-all(bf16[32,32,128]{2,1,0:T(8,128)(2,1)S(1)} %attend.1), channel_id=1, replica_groups={{0,128,256,384,400,272,144,16,32,160,288,416,432,304,176,48,64,192,320,..., dimensions={0} | all-to-all | bytes 524288 | tf_op jit(solution)/shard_map/all_to_all | solution.py:207
  59.0 1.0 %combine.1 = bf16[12,256]{1,0:T(8,128)(2,1)} custom-call(bf16[32,32,128]{2,1,0:T(8,128)(2,1)S(1)} %all_to_all.17.a_ref), custom_call_target="tpu_custom_call" | custom-call | tf_op jit(solution)/shard_map/combine/pallas_call | solution.py:264
Async XLA Ops:
  18.9 21.7 %copy-start = (bf16[1,8,128,1024]{3,2,1,0:T(8,128)(2,1)S(1)}, bf16[1,8,128,1024]{3,2,1,0:T(8,128)(2,1)}, u32[]{:S(2)}) copy-start(bf16[1,8,128,1024]{3,2,1,0:T(8,128)(2,1)} %param.6) | copy-start | bytes 6291460
  18.9 21.7 %copy-start.1 = (bf16[1,8,128,1024]{3,2,1,0:T(8,128)(2,1)S(1)}, bf16[1,8,128,1024]{3,2,1,0:T(8,128)(2,1)}, u32[]{:S(2)}) copy-start(bf16[1,8,128,1024]{3,2,1,0:T(8,128)(2,1)} %param.7) | copy-start | bytes 6291460
